TPU v7x, 16 devices: a whole 2x2x2 slice. The times are simulated.
16 devices in a mesh: row: 4 (over z, y), col: 4 (over x, core).
Axes of the slice: x: 2, y: 2, z: 2, core: 2. Of those that a mesh axis runs over, the one named last changes fastest.
Arguments:
- v_panels: float32 [8192, 8192], P('row', 'col')
- t_factors: float32 [128, 64, 64], P('col')
- z_vectors: float32 [8192, 2048], P(None, ('col', 'row'))
Outputs:
- output: float32 [8192, 2048], P('row', 'col')
All inputs are finite; a program needn't handle non-finite values.
Results may differ from a plain program's by a relative error of at most 0.001.
Values sent between devices are 32-bit elements.
A program may use at most 1 GiB of HBM per device.

v0:
```python
import jax
import jax.numpy as jnp
from jax import lax
from jax.sharding import PartitionSpec as P, NamedSharding

HIGHEST = lax.Precision.HIGHEST


def solution(mesh):
    col_devs = mesh.shape['col']

    def local_apply(v_loc, t_loc, z_loc):
        panel_width = t_loc.shape[1]
        groups = t_loc.shape[0]
        x_loc = lax.all_to_all(z_loc, 'row', 0, 1, tiled=True)

        def group_step(step_idx, x_cur):
            group_idx = groups - 1 - step_idx
            v_blk = lax.dynamic_slice_in_dim(v_loc, group_idx * panel_width, panel_width, axis=1)
            t_blk = lax.dynamic_index_in_dim(t_loc, group_idx, axis=0, keepdims=False)
            v_group = lax.all_gather(v_blk, 'col', axis=0)
            t_group = lax.all_gather(t_blk, 'col', axis=0)

            def panel_step(pos_idx, x_in):
                col_pos = col_devs - 1 - pos_idx
                v_j = lax.dynamic_index_in_dim(v_group, col_pos, axis=0, keepdims=False)
                t_j = lax.dynamic_index_in_dim(t_group, col_pos, axis=0, keepdims=False)
                w_part = jnp.einsum('na,nk->ak', v_j, x_in, precision=HIGHEST, preferred_element_type=jnp.float32)
                w_full = lax.psum(w_part, 'row')
                y_mat = jnp.dot(t_j, w_full, precision=HIGHEST, preferred_element_type=jnp.float32)
                return x_in - jnp.dot(v_j, y_mat, precision=HIGHEST, preferred_element_type=jnp.float32)

            return lax.fori_loop(0, col_devs, panel_step, x_cur)

        return lax.fori_loop(0, groups, group_step, x_loc)

    return jax.shard_map(local_apply, mesh=mesh,
                         in_specs=(P('row', 'col'), P('col', None, None), P(None, ('col', 'row'))),
                         out_specs=P('row', 'col'), check_vma=False)
```

profile of v0, /device:TPU:0, one launch (start us, length us, event | category | flops | bytes accessed | tf_op | source)
XLA Modules:
  0.0 7361.9 jit_solution(13559582478223341956)
XLA Ops:
  71.1 7283.9 %while.44 = (s32[]{:T(128)}, f32[2048,512]{1,0:T(8,128)}, f32[2048,2048]{1,0:T(8,128)}, f32[32,64,64]{2,1,0:T(8,128)}, s32[]{:T(128)}, /*index=5*/s32[]{:T(128)}...) while((s32[]{:T(128)}, f32[2048,512]{1,0:T(8,128)}, ...), condition=%wide.region_4.5_spmd, body=%wide.region_0.4_spmd.sunk | while | flops 1636859904 | bytes 27673112 | solution.py:35
  106.6 192.5 %while.45 = (s32[]{:T(128)}, f32[2048,512]{1,0:T(8,128)}, f32[4,2048,64]{2,1,0:T(8,128)}, f32[4,64,64]{2,1,0:T(8,128)S(1)}, s32[]{:T(128)}, /*index=5*/s32[]{:T(128)}, s32[]{:T(128)}, s32[]{:T(128)}) while((s32[]{:T(128)}, f32[2048,512]{1,0:T(8,128)}, f32[4,2048,64]{2,1,0:T(8,128)}, f32[4,64,64]{2,1,0:T(8,128)S(1)}, s32[]{:T(128)}, ...), condition=%wide.region_3.3_spmd, body=%wide.region_1.2_spmd.sunk | while | flops 1636859904 | bytes 16023735 | solution.py:33
  561.8 192.5 %while.45 = (s32[]{:T(128)}, f32[2048,512]{1,0:T(8,128)}, f32[4,2048,64]{2,1,0:T(8,128)}, f32[4,64,64]{2,1,0:T(8,128)S(1)}, s32[]{:T(128)}, /*index=5*/s32[]{:T(128)}, s32[]{:T(128)}, s32[]{:T(128)}) while((s32[]{:T(128)}, f32[2048,512]{1,0:T(8,128)}, f32[4,2048,64]{2,1,0:T(8,128)}, f32[4,64,64]{2,1,0:T(8,128)S(1)}, s32[]{:T(128)}, ...), condition=%wide.region_3.3_spmd, body=%wide.region_1.2_spmd.sunk | while | flops 1636859904 | bytes 16023735 | solution.py:33
  789.4 192.5 %while.45 = (s32[]{:T(128)}, f32[2048,512]{1,0:T(8,128)}, f32[4,2048,64]{2,1,0:T(8,128)}, f32[4,64,64]{2,1,0:T(8,128)S(1)}, s32[]{:T(128)}, /*index=5*/s32[]{:T(128)}, s32[]{:T(128)}, s32[]{:T(128)}) while((s32[]{:T(128)}, f32[2048,512]{1,0:T(8,128)}, f32[4,2048,64]{2,1,0:T(8,128)}, f32[4,64,64]{2,1,0:T(8,128)S(1)}, s32[]{:T(128)}, ...), condition=%wide.region_3.3_spmd, body=%wide.region_1.2_spmd.sunk | while | flops 1636859904 | bytes 16023735 | solution.py:33
  1017.0 192.5 %while.45 = (s32[]{:T(128)}, f32[2048,512]{1,0:T(8,128)}, f32[4,2048,64]{2,1,0:T(8,128)}, f32[4,64,64]{2,1,0:T(8,128)S(1)}, s32[]{:T(128)}, /*index=5*/s32[]{:T(128)}, s32[]{:T(128)}, s32[]{:T(128)}) while((s32[]{:T(128)}, f32[2048,512]{1,0:T(8,128)}, f32[4,2048,64]{2,1,0:T(8,128)}, f32[4,64,64]{2,1,0:T(8,128)S(1)}, s32[]{:T(128)}, ...), condition=%wide.region_3.3_spmd, body=%wide.region_1.2_spmd.sunk | while | flops 1636859904 | bytes 16023735 | solution.py:33
  1244.6 192.5 %while.45 = (s32[]{:T(128)}, f32[2048,512]{1,0:T(8,128)}, f32[4,2048,64]{2,1,0:T(8,128)}, f32[4,64,64]{2,1,0:T(8,128)S(1)}, s32[]{:T(128)}, /*index=5*/s32[]{:T(128)}, s32[]{:T(128)}, s32[]{:T(128)}) while((s32[]{:T(128)}, f32[2048,512]{1,0:T(8,128)}, f32[4,2048,64]{2,1,0:T(8,128)}, f32[4,64,64]{2,1,0:T(8,128)S(1)}, s32[]{:T(128)}, ...), condition=%wide.region_3.3_spmd, body=%wide.region_1.2_spmd.sunk | while | flops 1636859904 | bytes 16023735 | solution.py:33
  1472.3 192.5 %while.45 = (s32[]{:T(128)}, f32[2048,512]{1,0:T(8,128)}, f32[4,2048,64]{2,1,0:T(8,128)}, f32[4,64,64]{2,1,0:T(8,128)S(1)}, s32[]{:T(128)}, /*index=5*/s32[]{:T(128)}, s32[]{:T(128)}, s32[]{:T(128)}) while((s32[]{:T(128)}, f32[2048,512]{1,0:T(8,128)}, f32[4,2048,64]{2,1,0:T(8,128)}, f32[4,64,64]{2,1,0:T(8,128)S(1)}, s32[]{:T(128)}, ...), condition=%wide.region_3.3_spmd, body=%wide.region_1.2_spmd.sunk | while | flops 1636859904 | bytes 16023735 | solution.py:33
  1699.9 192.5 %while.45 = (s32[]{:T(128)}, f32[2048,512]{1,0:T(8,128)}, f32[4,2048,64]{2,1,0:T(8,128)}, f32[4,64,64]{2,1,0:T(8,128)S(1)}, s32[]{:T(128)}, /*index=5*/s32[]{:T(128)}, s32[]{:T(128)}, s32[]{:T(128)}) while((s32[]{:T(128)}, f32[2048,512]{1,0:T(8,128)}, f32[4,2048,64]{2,1,0:T(8,128)}, f32[4,64,64]{2,1,0:T(8,128)S(1)}, s32[]{:T(128)}, ...), condition=%wide.region_3.3_spmd, body=%wide.region_1.2_spmd.sunk | while | flops 1636859904 | bytes 16023735 | solution.py:33
  1927.5 192.5 %while.45 = (s32[]{:T(128)}, f32[2048,512]{1,0:T(8,128)}, f32[4,2048,64]{2,1,0:T(8,128)}, f32[4,64,64]{2,1,0:T(8,128)S(1)}, s32[]{:T(128)}, /*index=5*/s32[]{:T(128)}, s32[]{:T(128)}, s32[]{:T(128)}) while((s32[]{:T(128)}, f32[2048,512]{1,0:T(8,128)}, f32[4,2048,64]{2,1,0:T(8,128)}, f32[4,64,64]{2,1,0:T(8,128)S(1)}, s32[]{:T(128)}, ...), condition=%wide.region_3.3_spmd, body=%wide.region_1.2_spmd.sunk | while | flops 1636859904 | bytes 16023735 | solution.py:33
  2155.1 192.5 %while.45 = (s32[]{:T(128)}, f32[2048,512]{1,0:T(8,128)}, f32[4,2048,64]{2,1,0:T(8,128)}, f32[4,64,64]{2,1,0:T(8,128)S(1)}, s32[]{:T(128)}, /*index=5*/s32[]{:T(128)}, s32[]{:T(128)}, s32[]{:T(128)}) while((s32[]{:T(128)}, f32[2048,512]{1,0:T(8,128)}, f32[4,2048,64]{2,1,0:T(8,128)}, f32[4,64,64]{2,1,0:T(8,128)S(1)}, s32[]{:T(128)}, ...), condition=%wide.region_3.3_spmd, body=%wide.region_1.2_spmd.sunk | while | flops 1636859904 | bytes 16023735 | solution.py:33
  2382.7 192.5 %while.45 = (s32[]{:T(128)}, f32[2048,512]{1,0:T(8,128)}, f32[4,2048,64]{2,1,0:T(8,128)}, f32[4,64,64]{2,1,0:T(8,128)S(1)}, s32[]{:T(128)}, /*index=5*/s32[]{:T(128)}, s32[]{:T(128)}, s32[]{:T(128)}) while((s32[]{:T(128)}, f32[2048,512]{1,0:T(8,128)}, f32[4,2048,64]{2,1,0:T(8,128)}, f32[4,64,64]{2,1,0:T(8,128)S(1)}, s32[]{:T(128)}, ...), condition=%wide.region_3.3_spmd, body=%wide.region_1.2_spmd.sunk | while | flops 1636859904 | bytes 16023735 | solution.py:33
  2610.3 192.5 %while.45 = (s32[]{:T(128)}, f32[2048,512]{1,0:T(8,128)}, f32[4,2048,64]{2,1,0:T(8,128)}, f32[4,64,64]{2,1,0:T(8,128)S(1)}, s32[]{:T(128)}, /*index=5*/s32[]{:T(128)}, s32[]{:T(128)}, s32[]{:T(128)}) while((s32[]{:T(128)}, f32[2048,512]{1,0:T(8,128)}, f32[4,2048,64]{2,1,0:T(8,128)}, f32[4,64,64]{2,1,0:T(8,128)S(1)}, s32[]{:T(128)}, ...), condition=%wide.region_3.3_spmd, body=%wide.region_1.2_spmd.sunk | while | flops 1636859904 | bytes 16023735 | solution.py:33
  2837.9 192.5 %while.45 = (s32[]{:T(128)}, f32[2048,512]{1,0:T(8,128)}, f32[4,2048,64]{2,1,0:T(8,128)}, f32[4,64,64]{2,1,0:T(8,128)S(1)}, s32[]{:T(128)}, /*index=5*/s32[]{:T(128)}, s32[]{:T(128)}, s32[]{:T(128)}) while((s32[]{:T(128)}, f32[2048,512]{1,0:T(8,128)}, f32[4,2048,64]{2,1,0:T(8,128)}, f32[4,64,64]{2,1,0:T(8,128)S(1)}, s32[]{:T(128)}, ...), condition=%wide.region_3.3_spmd, body=%wide.region_1.2_spmd.sunk | while | flops 1636859904 | bytes 16023735 | solution.py:33
  3065.5 192.5 %while.45 = (s32[]{:T(128)}, f32[2048,512]{1,0:T(8,128)}, f32[4,2048,64]{2,1,0:T(8,128)}, f32[4,64,64]{2,1,0:T(8,128)S(1)}, s32[]{:T(128)}, /*index=5*/s32[]{:T(128)}, s32[]{:T(128)}, s32[]{:T(128)}) while((s32[]{:T(128)}, f32[2048,512]{1,0:T(8,128)}, f32[4,2048,64]{2,1,0:T(8,128)}, f32[4,64,64]{2,1,0:T(8,128)S(1)}, s32[]{:T(128)}, ...), condition=%wide.region_3.3_spmd, body=%wide.region_1.2_spmd.sunk | while | flops 1636859904 | bytes 16023735 | solution.py:33
  3293.2 192.5 %while.45 = (s32[]{:T(128)}, f32[2048,512]{1,0:T(8,128)}, f32[4,2048,64]{2,1,0:T(8,128)}, f32[4,64,64]{2,1,0:T(8,128)S(1)}, s32[]{:T(128)}, /*index=5*/s32[]{:T(128)}, s32[]{:T(128)}, s32[]{:T(128)}) while((s32[]{:T(128)}, f32[2048,512]{1,0:T(8,128)}, f32[4,2048,64]{2,1,0:T(8,128)}, f32[4,64,64]{2,1,0:T(8,128)S(1)}, s32[]{:T(128)}, ...), condition=%wide.region_3.3_spmd, body=%wide.region_1.2_spmd.sunk | while | flops 1636859904 | bytes 16023735 | solution.py:33
  3520.8 192.5 %while.45 = (s32[]{:T(128)}, f32[2048,512]{1,0:T(8,128)}, f32[4,2048,64]{2,1,0:T(8,128)}, f32[4,64,64]{2,1,0:T(8,128)S(1)}, s32[]{:T(128)}, /*index=5*/s32[]{:T(128)}, s32[]{:T(128)}, s32[]{:T(128)}) while((s32[]{:T(128)}, f32[2048,512]{1,0:T(8,128)}, f32[4,2048,64]{2,1,0:T(8,128)}, f32[4,64,64]{2,1,0:T(8,128)S(1)}, s32[]{:T(128)}, ...), condition=%wide.region_3.3_spmd, body=%wide.region_1.2_spmd.sunk | while | flops 1636859904 | bytes 16023735 | solution.py:33
  3748.4 192.5 %while.45 = (s32[]{:T(128)}, f32[2048,512]{1,0:T(8,128)}, f32[4,2048,64]{2,1,0:T(8,128)}, f32[4,64,64]{2,1,0:T(8,128)S(1)}, s32[]{:T(128)}, /*index=5*/s32[]{:T(128)}, s32[]{:T(128)}, s32[]{:T(128)}) while((s32[]{:T(128)}, f32[2048,512]{1,0:T(8,128)}, f32[4,2048,64]{2,1,0:T(8,128)}, f32[4,64,64]{2,1,0:T(8,128)S(1)}, s32[]{:T(128)}, ...), condition=%wide.region_3.3_spmd, body=%wide.region_1.2_spmd.sunk | while | flops 1636859904 | bytes 16023735 | solution.py:33
  3976.0 192.5 %while.45 = (s32[]{:T(128)}, f32[2048,512]{1,0:T(8,128)}, f32[4,2048,64]{2,1,0:T(8,128)}, f32[4,64,64]{2,1,0:T(8,128)S(1)}, s32[]{:T(128)}, /*index=5*/s32[]{:T(128)}, s32[]{:T(128)}, s32[]{:T(128)}) while((s32[]{:T(128)}, f32[2048,512]{1,0:T(8,128)}, f32[4,2048,64]{2,1,0:T(8,128)}, f32[4,64,64]{2,1,0:T(8,128)S(1)}, s32[]{:T(128)}, ...), condition=%wide.region_3.3_spmd, body=%wide.region_1.2_spmd.sunk | while | flops 1636859904 | bytes 16023735 | solution.py:33
  4203.6 192.5 %while.45 = (s32[]{:T(128)}, f32[2048,512]{1,0:T(8,128)}, f32[4,2048,64]{2,1,0:T(8,128)}, f32[4,64,64]{2,1,0:T(8,128)S(1)}, s32[]{:T(128)}, /*index=5*/s32[]{:T(128)}, s32[]{:T(128)}, s32[]{:T(128)}) while((s32[]{:T(128)}, f32[2048,512]{1,0:T(8,128)}, f32[4,2048,64]{2,1,0:T(8,128)}, f32[4,64,64]{2,1,0:T(8,128)S(1)}, s32[]{:T(128)}, ...), condition=%wide.region_3.3_spmd, body=%wide.region_1.2_spmd.sunk | while | flops 1636859904 | bytes 16023735 | solution.py:33
  4431.2 192.5 %while.45 = (s32[]{:T(128)}, f32[2048,512]{1,0:T(8,128)}, f32[4,2048,64]{2,1,0:T(8,128)}, f32[4,64,64]{2,1,0:T(8,128)S(1)}, s32[]{:T(128)}, /*index=5*/s32[]{:T(128)}, s32[]{:T(128)}, s32[]{:T(128)}) while((s32[]{:T(128)}, f32[2048,512]{1,0:T(8,128)}, f32[4,2048,64]{2,1,0:T(8,128)}, f32[4,64,64]{2,1,0:T(8,128)S(1)}, s32[]{:T(128)}, ...), condition=%wide.region_3.3_spmd, body=%wide.region_1.2_spmd.sunk | while | flops 1636859904 | bytes 16023735 | solution.py:33
  4658.8 192.5 %while.45 = (s32[]{:T(128)}, f32[2048,512]{1,0:T(8,128)}, f32[4,2048,64]{2,1,0:T(8,128)}, f32[4,64,64]{2,1,0:T(8,128)S(1)}, s32[]{:T(128)}, /*index=5*/s32[]{:T(128)}, s32[]{:T(128)}, s32[]{:T(128)}) while((s32[]{:T(128)}, f32[2048,512]{1,0:T(8,128)}, f32[4,2048,64]{2,1,0:T(8,128)}, f32[4,64,64]{2,1,0:T(8,128)S(1)}, s32[]{:T(128)}, ...), condition=%wide.region_3.3_spmd, body=%wide.region_1.2_spmd.sunk | while | flops 1636859904 | bytes 16023735 | solution.py:33
  4886.4 192.5 %while.45 = (s32[]{:T(128)}, f32[2048,512]{1,0:T(8,128)}, f32[4,2048,64]{2,1,0:T(8,128)}, f32[4,64,64]{2,1,0:T(8,128)S(1)}, s32[]{:T(128)}, /*index=5*/s32[]{:T(128)}, s32[]{:T(128)}, s32[]{:T(128)}) while((s32[]{:T(128)}, f32[2048,512]{1,0:T(8,128)}, f32[4,2048,64]{2,1,0:T(8,128)}, f32[4,64,64]{2,1,0:T(8,128)S(1)}, s32[]{:T(128)}, ...), condition=%wide.region_3.3_spmd, body=%wide.region_1.2_spmd.sunk | while | flops 1636859904 | bytes 16023735 | solution.py:33
  5114.1 192.5 %while.45 = (s32[]{:T(128)}, f32[2048,512]{1,0:T(8,128)}, f32[4,2048,64]{2,1,0:T(8,128)}, f32[4,64,64]{2,1,0:T(8,128)S(1)}, s32[]{:T(128)}, /*index=5*/s32[]{:T(128)}, s32[]{:T(128)}, s32[]{:T(128)}) while((s32[]{:T(128)}, f32[2048,512]{1,0:T(8,128)}, f32[4,2048,64]{2,1,0:T(8,128)}, f32[4,64,64]{2,1,0:T(8,128)S(1)}, s32[]{:T(128)}, ...), condition=%wide.region_3.3_spmd, body=%wide.region_1.2_spmd.sunk | while | flops 1636859904 | bytes 16023735 | solution.py:33
  6935.0 192.5 %while.45 = (s32[]{:T(128)}, f32[2048,512]{1,0:T(8,128)}, f32[4,2048,64]{2,1,0:T(8,128)}, f32[4,64,64]{2,1,0:T(8,128)S(1)}, s32[]{:T(128)}, /*index=5*/s32[]{:T(128)}, s32[]{:T(128)}, s32[]{:T(128)}) while((s32[]{:T(128)}, f32[2048,512]{1,0:T(8,128)}, f32[4,2048,64]{2,1,0:T(8,128)}, f32[4,64,64]{2,1,0:T(8,128)S(1)}, s32[]{:T(128)}, ...), condition=%wide.region_3.3_spmd, body=%wide.region_1.2_spmd.sunk | while | flops 1636859904 | bytes 16023735 | solution.py:33
  (973 shorter events, 9077.9 us)
Async XLA Ops:
  6.5 53.8 all-to-all-start
  202.8 40.1 all-reduce.2.cloned.1.call-start
  478.5 40.1 all-reduce.2.cloned.1.call-start
  706.1 40.1 all-reduce.2.cloned.1.call-start
  933.7 40.1 all-reduce.2.cloned.1.call-start
  1161.4 40.1 all-reduce.2.cloned.1.call-start
  1389.0 40.1 all-reduce.2.cloned.1.call-start
  1616.6 40.1 all-reduce.2.cloned.1.call-start
  1844.2 40.1 all-reduce.2.cloned.1.call-start
  2071.8 40.1 all-reduce.2.cloned.1.call-start
  2299.4 40.1 all-reduce.2.cloned.1.call-start
  2527.0 40.1 all-reduce.2.cloned.1.call-start
  2754.7 40.1 all-reduce.2.cloned.1.call-start
  2982.3 40.1 all-reduce.2.cloned.1.call-start
  3209.9 40.1 all-reduce.2.cloned.1.call-start
  3437.5 40.1 all-reduce.2.cloned.1.call-start
  3665.1 40.1 all-reduce.2.cloned.1.call-start
  3892.7 40.1 all-reduce.2.cloned.1.call-start
  4120.3 40.1 all-reduce.2.cloned.1.call-start
  4347.9 40.1 all-reduce.2.cloned.1.call-start
  4575.6 40.1 all-reduce.2.cloned.1.call-start
  4803.2 40.1 all-reduce.2.cloned.1.call-start
  5030.8 40.1 all-reduce.2.cloned.1.call-start
  6396.5 40.1 all-reduce.2.cloned.1.call-start
  (137 other events, 5338.6 us)
Sparse Core Ops, SparseCore 0:
  484.2 34.4 all-reduce.1
  711.8 34.4 all-reduce.1
  939.4 34.4 all-reduce.1
  1167.0 34.4 all-reduce.1
  1394.6 34.4 all-reduce.1
  1622.3 34.4 all-reduce.1
  1849.9 34.4 all-reduce.1
  2077.5 34.4 all-reduce.1
  2305.1 34.4 all-reduce.1
  2532.7 34.4 all-reduce.1
  2760.3 34.4 all-reduce.1
  2987.9 34.4 all-reduce.1
  3215.5 34.4 all-reduce.1
  3443.2 34.4 all-reduce.1
  3670.8 34.4 all-reduce.1
  3898.4 34.4 all-reduce.1
  4126.0 34.4 all-reduce.1
  4353.6 34.4 all-reduce.1
  4581.2 34.4 all-reduce.1
  4808.8 34.4 all-reduce.1
  5036.4 34.4 all-reduce.1
  5264.1 34.4 all-reduce.1
  5491.7 34.4 all-reduce.1
  5719.3 34.4 all-reduce.1
  (136 shorter events, 4610.3 us)
where the time goes:
time: 7370 us; the launch traced here: 7360 us
  waiting for transfers between devices  5320 us (72%)
  matrix products  1730 us (23%)
  blocking collectives  173 us (2%)
  local copies, waits for them, and re-layouts  116 us (2%)
    psum x128, waiting for transfers between devices, panel_step(): w_full = lax.psum(w_part, 'row')  4430 us
    dot_general x128, matrix products, panel_step(): jnp.dot(v_j, y_mat, precision=HIGHEST, preferred_element_type=jnp.float32)  872 us
    all_gather x32, waiting for transfers between devices, group_step(): v_group = lax.all_gather(v_blk, 'col', axis=0)  845 us
    dot_general x128, matrix products, panel_step(): jnp.einsum('na,nk->ak', v_j, x_in, precision=HIGHEST, preferred_element_t...  706 us
    all_gather x32, blocking collectives, group_step(): t_group = lax.all_gather(t_blk, 'col', axis=0)  173 us
    dot_general x128, matrix products, panel_step(): jnp.dot(t_j, w_full, precision=HIGHEST, preferred_element_type=jnp.float32)  149 us
  transfers between devices with their start and end apart: 161, of which 161 were waited for; matrix products, arithmetic and copies ran while one was open for 0% of the time, Pallas kernels for 0%

commit v1 on v0

v1 whole, which is shorter than its diff:
```python
import jax
import jax.numpy as jnp
from jax import lax
from jax.experimental import pallas as pl
from jax.experimental.pallas import tpu as pltpu
from jax.sharding import PartitionSpec as P

F32 = jnp.float32
BF16 = jnp.bfloat16
MESH = pl.DeviceIdType.MESH
NBLK = 16
AHEAD = 4
NT = (((1,), (1,)), ((), ()))
NN = (((1,), (0,)), ((), ()))


def split3(val):
    high = val.astype(BF16)
    rest = val - high.astype(F32)
    mid = rest.astype(BF16)
    low = (rest - mid.astype(F32)).astype(BF16)
    return high, mid, low


def stack3(val):
    return jnp.concatenate(split3(val), axis=0)


def dot6(stack, b_high, b_mid, b_low, dims):
    rows = stack.shape[0] // 3
    o_high = lax.dot_general(stack, b_high, dims, preferred_element_type=F32)
    o_mid = lax.dot_general(stack[:2 * rows], b_mid, dims, preferred_element_type=F32)
    o_low = lax.dot_general(stack[:rows], b_low, dims, preferred_element_type=F32)
    small = (o_high[2 * rows:] + o_mid[rows:]) + o_low
    return o_high[:rows] + ((o_high[rows:2 * rows] + o_mid[:rows]) + small)


def kernel(v, tt, z4, o, vb, zb, vp, xt, stage, zst, tbv, ts, tp, ys, wsend, wrecv, gsend, grecv, osb,
           v_s, v_r, z_s, z_r, zl, tb_s, tb_r, tb_l, t_s, t_r, w_s, w_r, g_s, g_r, st_a, st_b, o_s, o_r, o_l):
    r = lax.axis_index('row')
    c = lax.axis_index('col')
    zz, yy, xx, kk = r // 2, r % 2, c // 2, c % 2
    dev_x = (r, (1 - xx) * 2 + kk)
    dev_y = (zz * 2 + (1 - yy), c)
    dev_z = ((1 - zz) * 2 + yy, c)
    dev_p = (r, xx * 2 + (1 - kk))
    dev_d = (zz * 2 + yy + (1 - kk) * (1 - 2 * yy), (xx + kk * (1 - 2 * xx)) * 2 + kk)

    barrier = pltpu.get_barrier_semaphore()
    for dev in (dev_x, dev_y, dev_z, dev_p):
        pl.semaphore_signal(barrier, 1, device_id=dev, device_id_type=MESH)
    pl.semaphore_wait(barrier, 4)

    def remote(src, dst, s_sem, r_sem, dev):
        return pltpu.make_async_remote_copy(src_ref=src, dst_ref=dst, send_sem=s_sem, recv_sem=r_sem,
                                            device_id=dev, device_id_type=MESH)

    def own(qq, idx, dev):
        r0 = 128 * qq
        return remote(v.at[pl.ds(r0, 2048 - r0), pl.ds(r0, 128)], vb.at[qq, idx, pl.ds(r0, 2048 - r0)],
                      v_s.at[qq, idx], v_r.at[qq, idx], dev)

    def fwd(qq, src, idx, dev):
        r0 = 128 * qq
        return remote(vb.at[qq, src, pl.ds(r0, 2048 - r0)], vb.at[qq, idx, pl.ds(r0, 2048 - r0)],
                      v_s.at[qq, idx], v_r.at[qq, idx], dev)

    def slab(qq, idx):
        if idx in (0, 1, 3):
            return own(qq, idx, {0: dev_p, 1: dev_x, 3: dev_y}[idx])
        if idx == 5:
            return fwd(qq, 1 + 2 * kk, 5, dev_d)
        return fwd(qq, idx - 1, idx, dev_p)

    def at_q(q, fn):
        for qq in range(NBLK):
            @pl.when(q == qq)
            def _():
                fn(qq)

    def send_own(qq):
        for idx in (1, 3, 0):
            slab(qq, idx).start()

    def pass_on(qq):
        for idx in (1, 3):
            slab(qq, idx).wait_recv()
        for idx in (5, 2, 4):
            slab(qq, idx).start()

    def pass_diag(qq):
        slab(qq, 5).wait_recv()
        slab(qq, 6).start()

    def all_here(qq):
        for idx in (0, 2, 4, 6):
            slab(qq, idx).wait_recv()

    def z_copy(ch):
        rows = pl.ds(pl.multiple_of(256 * ch, 256), 256)
        return remote(z4.at[pl.ds(2 * (1 - zz), 2), rows], zb.at[:, rows], z_s.at[ch], z_r.at[ch], dev_z)

    def z_loads(ch):
        rows = pl.ds(pl.multiple_of(256 * ch, 256), 256)
        return (pltpu.make_async_copy(z4.at[pl.ds(2 * zz, 2), rows], zst.at[zz], zl.at[0]),
                pltpu.make_async_copy(zb.at[:, rows], zst.at[1 - zz], zl.at[1]))

    halves = ((12, 4), (0, 12))

    def t_copy(half, way):
        q0, nq = halves[half]
        part = pl.ds(q0, nq)
        src = tbv.at[2, part] if way == 2 else tt.at[part]
        return remote(src, tbv.at[way + 1, part], tb_s.at[half, way], tb_r.at[half, way],
                      dev_x if way == 1 else dev_p)

    def w_copy(s, par):
        return remote(wsend.at[s, par], wrecv.at[s, par], w_s.at[s, par], w_r.at[s, par], dev_z)

    def g_copy(slot):
        return remote(gsend.at[slot], grecv.at[slot], g_s.at[slot], g_r.at[slot], dev_z)

    def s_copy(slot):
        return remote(ts.at[slot, kk], ts.at[slot, kk], t_s.at[slot], t_r.at[slot], dev_p)

    own_t = pltpu.make_async_copy(tt, tbv.at[0], tb_l)
    own_t.start()
    for way in range(2):
        t_copy(0, way).start()
    send_own(15)
    z_copy(7).start()
    send_own(14)
    z_copy(6).start()
    send_own(13)
    for way in range(2):
        t_copy(1, way).start()
    own_t.wait()

    lane = lax.broadcasted_iota(jnp.int32, (128, 128), 1)
    left = lane < 64
    left64 = left[:64]

    def stage_loads(q, ch, buf):
        rows = pl.ds(pl.multiple_of(256 * ch, 256), 256)
        cols = pl.ds(pl.multiple_of(128 * q, 128), 128)
        return (pltpu.make_async_copy(v.at[rows, cols], stage.at[buf, 0], st_a.at[buf]),
                pltpu.make_async_copy(vb.at[q, :, rows], stage.at[buf, pl.ds(1, 7)], st_b.at[buf]))

    def prepare(qn, slot):
        cq = qn // 2
        n = 8 - cq
        gsend[slot] = jnp.zeros((192, 256), F32)
        for cp in stage_loads(qn, 7, 0):
            cp.start()

        def chunk(j, _):
            ch = 7 - j
            buf = j % 2

            @pl.when(j + 1 < n)
            def _():
                for cp in stage_loads(qn, ch - 1, 1 - buf):
                    cp.start()

            for cp in stage_loads(qn, ch, buf):
                cp.wait()
            empty = (qn % 2 == 1) & (ch == cq)
            for y1 in range(2):
                dy = (y1 + yy) % 2
                for h in range(2):
                    for pair in range(2):
                        dx = (pair + xx) % 2
                        rel = dy * 4 + dx * 2
                        a0 = stage[buf, rel + kk, pl.ds(128 * h, 128), :]
                        a1 = stage[buf, rel + 1 - kk, pl.ds(128 * h, 128), :]
                        if h == 0:
                            a0 = jnp.where(empty, 0.0, a0)
                            a1 = jnp.where(empty, 0.0, a1)
                        r0 = pltpu.roll(a0, 64, 1)
                        r1 = pltpu.roll(a1, 64, 1)
                        vals = (jnp.where(left, a0, r1), jnp.where(left, r0, a1))
                        for par in range(2):
                            parts = split3(vals[par])
                            for piece in range(3):
                                vp[slot, par, piece, ch, pl.ds(y1 * 256 + h * 128, 128),
                                   pl.ds(pair * 128, 128)] = parts[piece]
            vh = vp[slot, kk, 0, ch]
            vm = vp[slot, kk, 1, ch]
            vl = vp[slot, kk, 2, ch]
            lhs = jnp.concatenate([vh.T[64:], vm.T[64:], vl.T[64:]], axis=0)
            gsend[slot] += dot6(lhs, vh, vm, vl, NN)
            return 0

        lax.fori_loop(0, n, chunk, 0)

    def form_t(qn, slot):
        zero = jnp.zeros((64, 128), F32)
        rows = []
        for e in range(4):
            dx = (e // 2 + xx) % 2
            dk = (e % 2 + kk) % 2
            val = tbv[dx * 2 + dk, qn]
            other = pltpu.roll(val, 64, 1)
            if e % 2 == 0:
                piece = jnp.where(left64, jnp.where(kk == 0, val, other), 0.0)
            else:
                piece = jnp.where(left64, 0.0, jnp.where(kk == 0, other, val))
            rows.append(jnp.concatenate([piece, zero] if e < 2 else [zero, piece], axis=1))
        s0 = jnp.concatenate(rows, axis=0)
        gram = jnp.concatenate([jnp.zeros((64, 256), F32), gsend[slot] + grecv[slot]], axis=0)
        bi = lax.broadcasted_iota(jnp.int32, (256, 256), 0) // 64
        bj = lax.broadcasted_iota(jnp.int32, (256, 256), 1) // 64
        near = ((bi == 1) & (bj == 0)) | ((bi == 3) & (bj == 2))
        far = (bi >= 2) & (bj < 2)
        for mask in (near, far):
            gm = split3(jnp.where(mask, gram, 0.0))
            sp = split3(s0)
            st = jnp.concatenate(sp, axis=0)
            mid = dot6(st, *gm, NN)
            s0 = s0 - dot6(stack3(mid), *sp, NN)
        ts[slot, kk] = s0

    def update(s, slot, par, ch):
        yst = ys[...]
        delta = dot6(yst, vp[slot, par, 0, ch], vp[slot, par, 1, ch], vp[slot, par, 2, ch], NT)
        new = xt[s, ch] - delta
        xt[s, ch] = new
        return new

    def project(s, slot, par, ch, into):
        wsend[s, into] += dot6(stack3(xt[s, ch]), vp[slot, par, 0, ch], vp[slot, par, 1, ch], vp[slot, par, 2, ch], NN)

    def out_copies(s, ch):
        rows = pl.ds(pl.multiple_of(256 * ch, 256), 256)
        cols = pl.ds(pl.multiple_of((2 * s + yy) * 128, 128), 128)
        return (pltpu.make_async_copy(osb.at[s, ch, yy], o.at[rows, cols], o_l.at[s, ch]),
                remote(osb.at[s, ch, 1 - yy], o.at[rows, cols], o_s.at[s, ch], o_r.at[s, ch], dev_y))

    def step(g, _):
        i = g // 4 - 1
        sub = g % 4
        q = 15 - i
        qn = 14 - i
        par = 1 - sub // 2
        s = sub % 2
        cur = (i + 2) % 2
        nxt = (i + 1) % 2
        more = i < 15

        @pl.when((sub == 0) & more)
        def _():
            at_q(qn, pass_on)

            @pl.when(i + AHEAD < NBLK)
            def _():
                at_q(15 - (i + AHEAD), send_own)

            @pl.when(qn % 2 == 1)
            def _():
                ch = qn // 2

                @pl.when(ch >= 2)
                def _():
                    z_copy(ch - 2).start()
                z_copy(ch).wait_recv()
                for cp in z_loads(ch):
                    cp.start()

        @pl.when(g == 0)
        def _():
            t_copy(0, 1).wait_recv()
            t_copy(0, 2).start()

        @pl.when(g == 3)
        def _():
            t_copy(0, 0).wait_recv()
            t_copy(0, 2).wait_recv()

        @pl.when(g == 5)
        def _():
            t_copy(1, 1).wait_recv()
            t_copy(1, 2).start()

        @pl.when(g == 9)
        def _():
            t_copy(1, 0).wait_recv()
            t_copy(1, 2).wait_recv()

        @pl.when((sub == 0) & (i >= 0))
        def _():
            s_copy(cur).wait()
            for pp in range(2):
                for piece, val in enumerate(split3(ts[cur, pp])):
                    tp[pp, piece] = val

        @pl.when((sub == 1) & more)
        def _():
            at_q(qn, pass_diag)

        @pl.when((sub == 2) & more)
        def _():
            at_q(qn, all_here)
            prepare(qn, nxt)
            g_copy(nxt).start()

            @pl.when(qn % 2 == 1)
            def _():
                ch = qn // 2
                for cp in z_loads(ch):
                    cp.wait()
                for ss in range(2):
                    for y1 in range(2):
                        xt[ss, ch, :, pl.ds(y1 * 256, 256)] = zst[ss, y1].T

        @pl.when((sub == 3) & more)
        def _():
            g_copy(nxt).wait()
            form_t(qn, nxt)
            s_copy(nxt).start()

        has_u = i >= 0
        has_w = ((i < 15) | (sub < 2)) & ((i >= 0) | (sub >= 2))
        n = 8 - q // 2
        w_par = 1 - par
        w_slot = jnp.where(sub < 2, cur, nxt)
        n_w = jnp.where(sub < 2, n, 8 - qn // 2)

        @pl.when(has_u)
        def _():
            w_copy(s, par).wait()
            w_sum = wsend[s, par] + wrecv[s, par]
            y_val = dot6(stack3(w_sum), tp[par, 0], tp[par, 1], tp[par, 2], NN)
            ys[...] = stack3(y_val)

        @pl.when(has_w)
        def _():
            wsend[s, w_par] = jnp.zeros((128, 256), F32)

        @pl.when(has_u & has_w)
        def _():
            update(s, cur, par, 7)

            def both(j, _):
                update(s, cur, par, 7 - j)
                project(s, w_slot, w_par, 8 - j, w_par)
                return 0
            lax.fori_loop(1, n, both, 0)

        @pl.when(has_w)
        def _():
            def rest(j, _):
                project(s, w_slot, w_par, 7 - j, w_par)
                return 0
            lax.fori_loop(jnp.where(has_u, n - 1, 0), n_w, rest, 0)
            w_copy(s, w_par).start()

        @pl.when(has_u & jnp.logical_not(has_w))
        def _():
            def last(j, _):
                ch = 7 - j
                new = update(s, cur, par, ch)
                for y1 in range(2):
                    osb[s, ch, y1] = new[:, y1 * 256:(y1 + 1) * 256].T
                for cp in out_copies(s, ch):
                    cp.start()
                return 0
            lax.fori_loop(0, 8, last, 0)
        return 0

    lax.fori_loop(0, 4 * (NBLK + 1), step, 0)

    for half in range(2):
        for way in range(3):
            t_copy(half, way).wait_send()
    for qq in range(NBLK):
        for idx in range(7):
            slab(qq, idx).wait_send()

    def drain(ch, _):
        z_copy(ch).wait_send()
        for s in range(2):
            local, far = out_copies(s, ch)
            local.wait()
            far.wait()
        return 0
    lax.fori_loop(0, 8, drain, 0)


def solution(mesh):
    def local_apply(v_loc, t_loc, z_loc):
        tt = jnp.swapaxes(t_loc, 1, 2).reshape(NBLK, 2, 64, 64).transpose(0, 2, 1, 3).reshape(NBLK, 64, 128)
        z4 = z_loc.reshape(4, 2048, 128)
        any_spec = pl.BlockSpec(memory_space=pl.ANY)
        dma, vmem = pltpu.SemaphoreType.DMA, pltpu.VMEM
        out = pl.pallas_call(
            kernel,
            out_shape=(jax.ShapeDtypeStruct((2048, 512), F32),
                       jax.ShapeDtypeStruct((NBLK, 7, 2048, 128), F32),
                       jax.ShapeDtypeStruct((2, 2048, 128), F32)),
            in_specs=[any_spec] * 3,
            out_specs=(any_spec,) * 3,
            scratch_shapes=[
                vmem((2, 2, 3, 8, 512, 256), BF16),
                vmem((2, 8, 128, 512), F32),
                vmem((2, 8, 256, 128), F32),
                vmem((2, 2, 256, 128), F32),
                vmem((4, NBLK, 64, 128), F32),
                vmem((2, 2, 256, 256), F32),
                vmem((2, 3, 256, 256), BF16),
                vmem((384, 256), BF16),
                vmem((2, 2, 128, 256), F32),
                vmem((2, 2, 128, 256), F32),
                vmem((2, 192, 256), F32),
                vmem((2, 192, 256), F32),
                vmem((2, 8, 2, 256, 128), F32),
                dma((NBLK, 7)), dma((NBLK, 7)),
                dma((8,)), dma((8,)), dma((2,)),
                dma((2, 3)), dma((2, 3)), dma,
                dma((2,)), dma((2,)),
                dma((2, 2)), dma((2, 2)),
                dma((2,)), dma((2,)),
                dma((2,)), dma((2,)),
                dma((2, 8)), dma((2, 8)), dma((2, 8)),
            ],
            compiler_params=pltpu.CompilerParams(collective_id=0, has_side_effects=True, vmem_limit_bytes=64_000_000),
        )(v_loc, tt, z4)
        return out[0]

    return jax.shard_map(local_apply, mesh=mesh,
                         in_specs=(P('row', 'col'), P('col', None, None), P(None, ('col', 'row'))),
                         out_specs=P('row', 'col'), check_vma=False)
```

time: 7370 us -> 640 us (0.09)
  waiting for transfers between devices: 5320 us -> 0 us
  matrix products: 1730 us -> 0 us
  Pallas kernels: 0 us -> 631 us
  blocking collectives: 173 us -> 0 us
  local copies, waits for them, and re-layouts: 116 us -> 7.61 us
    psum x128 -> x0, waiting for transfers between devices: 4430 us -> none  [panel_step(): w_full = lax.psum(w_part, 'row')]
    dot_general x384 -> x0, matrix products: 1730 us -> none  [the longest x128 872 us: panel_step(): jnp.dot(v_j, y_mat, precision=HIGHEST, preferred_element_type=jnp.float32)]
    all_gather x32 -> x0, waiting for transfers between devices: 845 us -> none  [group_step(): v_group = lax.all_gather(v_blk, 'col', axis=0)]
    pallas_call x0 -> x1, Pallas kernels: none -> 631 us  [local_apply(): pl.pallas_call(kernel, out_shape=(jax.ShapeDtypeStruct((2048, 512), F32),...]
    all_gather x32 -> x0, blocking collectives: 173 us -> none  [group_step(): t_group = lax.all_gather(t_blk, 'col', axis=0)]
    dynamic_slice x64 -> x0, local copies, waits for them, and re-layouts: 105 us -> none  [the longest x32 81 us: group_step(): lax.dynamic_slice_in_dim(v_loc, group_idx * panel_width, panel_width, axi...]
  transfers between devices with their start and end apart: 161 -> 0, of which waited for: 161 -> 0; matrix products, arithmetic and copies ran while one was open for 0% -> 0% of each run, Pallas kernels for 0% -> 0%
where the time goes in v1:
time: 640 us; the launch traced here: 638 us
  Pallas kernels  631 us (99%)
  local copies, waits for them, and re-layouts  7.61 us (1%)
    pallas_call x1, Pallas kernels, local_apply(): pl.pallas_call(kernel, out_shape=(jax.ShapeDtypeStruct((2048, 512), F32),...  631 us

profile of v1, /device:TPU:0, one launch (start us, length us, event | category | flops | bytes accessed | tf_op | source)
XLA Modules:
  0.0 638.3 jit_solution(8474060856194689363)
XLA Ops:
  0.0 1.6 copy.4
  1.6 1.4 reshape.10.tt
  3.0 630.7 %shard_map.37 = (f32[2048,512]{1,0:T(8,128)}, f32[16,7,2048,128]{3,2,1,0:T(8,128)}, f32[2,2048,128]{2,1,0:T(8,128)}) custom-call(f32[2048,2048]{1,0:T(8,128)} %v.1, f32[16,64,128]{2,1,0:T(8,128)} %reshape.10.tt, f32[4,2048,128]{2,1,0:T(8,128)} %bitcast.6), custom_call_target="tpu_custom_call" | custom-call | tf_op jit(solution)/shard_map/pallas_call | solution.py:395
  633.7 4.6 copy.6

commit v2 on v1

--- a/solution.py
+++ b/solution.py
@@ -9,7 +9,6 @@
 BF16 = jnp.bfloat16
 MESH = pl.DeviceIdType.MESH
 NBLK = 16
-AHEAD = 4
 NT = (((1,), (1,)), ((), ()))
 NN = (((1,), (0,)), ((), ()))
 
@@ -35,7 +34,25 @@
     return o_high[:rows] + ((o_high[rows:2 * rows] + o_mid[:rows]) + small)
 
 
-def kernel(v, tt, z4, o, vb, zb, vp, xt, stage, zst, tbv, ts, tp, ys, wsend, wrecv, gsend, grecv, osb,
+def v_table():
+    table = {}
+
+    def add(trip, quarter, what, blk):
+        if 0 <= blk < NBLK:
+            table.setdefault((trip, quarter), []).append((what, blk))
+
+    for trip in range(-1, NBLK):
+        if trip >= 0:
+            add(trip, 0, 'fwd', trip + 4)
+            add(trip, 2, 'diag', trip + 3)
+        add(trip, 0, 'own', trip + 6)
+        add(trip, 3, 'here', trip + 2)
+    for quarter, what, blk in ((1, 'fwd', 2), (1, 'diag', 1), (2, 'fwd', 3), (3, 'diag', 2)):
+        table.setdefault((-1, quarter), []).insert(0, (what, blk))
+    return table
+
+
+def kernel(v, tt, z4, o, vb, zb, vp, xt, stage, zst, tbv, ts, tp, ys, wsend, wrecv, gacc, gsend, grecv, osb,
            v_s, v_r, z_s, z_r, zl, tb_s, tb_r, tb_l, t_s, t_r, w_s, w_r, g_s, g_r, st_a, st_b, o_s, o_r, o_l):
     r = lax.axis_index('row')
     c = lax.axis_index('col')
@@ -55,6 +72,9 @@
         return pltpu.make_async_remote_copy(src_ref=src, dst_ref=dst, send_sem=s_sem, recv_sem=r_sem,
                                             device_id=dev, device_id_type=MESH)
 
+    def mult(val, by):
+        return val if isinstance(val, int) else pl.multiple_of(val, by)
+
     def own(qq, idx, dev):
         r0 = 128 * qq
         return remote(v.at[pl.ds(r0, 2048 - r0), pl.ds(r0, 128)], vb.at[qq, idx, pl.ds(r0, 2048 - r0)],
@@ -72,11 +92,16 @@
             return fwd(qq, 1 + 2 * kk, 5, dev_d)
         return fwd(qq, idx - 1, idx, dev_p)
 
-    def at_q(q, fn):
-        for qq in range(NBLK):
-            @pl.when(q == qq)
-            def _():
-                fn(qq)
+    def at_trip(i, table):
+        for first in range(-1, NBLK, 4):
+            mine = [t for t in range(first, first + 4) if t in table]
+            if mine:
+                @pl.when((i >= first) & (i < first + 4))
+                def _():
+                    for trip in mine:
+                        @pl.when(i == trip)
+                        def _():
+                            table[trip]()
 
     def send_own(qq):
         for idx in (1, 3, 0):
@@ -92,9 +117,26 @@
         slab(qq, 5).wait_recv()
         slab(qq, 6).start()
 
+    def stage_loads(q, ch, buf):
+        rows = pl.ds(mult(256 * ch, 256), 256)
+        cols = pl.ds(mult(128 * q, 128), 128)
+        return (pltpu.make_async_copy(v.at[rows, cols], stage.at[buf, 0], st_a.at[buf]),
+                pltpu.make_async_copy(vb.at[q, :, rows], stage.at[buf, pl.ds(1, 7)], st_b.at[buf]))
+
     def all_here(qq):
         for idx in (0, 2, 4, 6):
             slab(qq, idx).wait_recv()
+        for j in range(min(2, 8 - qq // 2)):
+            for cp in stage_loads(qq, 7 - j, j):
+                cp.start()
+
+    do = {'own': send_own, 'fwd': pass_on, 'diag': pass_diag, 'here': all_here}
+
+    def run_of(events):
+        def run():
+            for what, blk in events:
+                do[what](15 - blk)
+        return run
 
     def z_copy(ch):
         rows = pl.ds(pl.multiple_of(256 * ch, 256), 256)
@@ -125,45 +167,41 @@
 
     own_t = pltpu.make_async_copy(tt, tbv.at[0], tb_l)
     own_t.start()
+    send_own(15)
+    send_own(14)
     for way in range(2):
         t_copy(0, way).start()
-    send_own(15)
     z_copy(7).start()
-    send_own(14)
     z_copy(6).start()
     send_own(13)
+    pass_on(15)
+    pass_on(14)
+    send_own(12)
+    pass_diag(15)
+    send_own(11)
     for way in range(2):
         t_copy(1, way).start()
     own_t.wait()
+    all_here(15)
 
     lane = lax.broadcasted_iota(jnp.int32, (128, 128), 1)
     left = lane < 64
     left64 = left[:64]
 
-    def stage_loads(q, ch, buf):
-        rows = pl.ds(pl.multiple_of(256 * ch, 256), 256)
-        cols = pl.ds(pl.multiple_of(128 * q, 128), 128)
-        return (pltpu.make_async_copy(v.at[rows, cols], stage.at[buf, 0], st_a.at[buf]),
-                pltpu.make_async_copy(vb.at[q, :, rows], stage.at[buf, pl.ds(1, 7)], st_b.at[buf]))
-
     def prepare(qn, slot):
         cq = qn // 2
         n = 8 - cq
-        gsend[slot] = jnp.zeros((192, 256), F32)
-        for cp in stage_loads(qn, 7, 0):
-            cp.start()
-
-        def chunk(j, _):
+        gacc[...] = jnp.zeros((192, 256), F32)
+
+        def take(j):
             ch = 7 - j
             buf = j % 2
-
-            @pl.when(j + 1 < n)
-            def _():
-                for cp in stage_loads(qn, ch - 1, 1 - buf):
-                    cp.start()
-
             for cp in stage_loads(qn, ch, buf):
                 cp.wait()
+
+        def parts(j):
+            ch = 7 - j
+            buf = j % 2
             empty = (qn % 2 == 1) & (ch == cq)
             for y1 in range(2):
                 dy = (y1 + yy) % 2
@@ -180,45 +218,66 @@
                         r1 = pltpu.roll(a1, 64, 1)
                         vals = (jnp.where(left, a0, r1), jnp.where(left, r0, a1))
                         for par in range(2):
-                            parts = split3(vals[par])
-                            for piece in range(3):
+                            for piece, val in enumerate(split3(vals[par])):
                                 vp[slot, par, piece, ch, pl.ds(y1 * 256 + h * 128, 128),
-                                   pl.ds(pair * 128, 128)] = parts[piece]
-            vh = vp[slot, kk, 0, ch]
-            vm = vp[slot, kk, 1, ch]
-            vl = vp[slot, kk, 2, ch]
+                                   pl.ds(pair * 128, 128)] = val
+
+        def more_loads(j):
+            @pl.when(j + 2 < n)
+            def _():
+                for cp in stage_loads(qn, 5 - j, j % 2):
+                    cp.start()
+
+        def gram(j):
+            vh, vm, vl = (vp[slot, kk, piece, 7 - j] for piece in range(3))
             lhs = jnp.concatenate([vh.T[64:], vm.T[64:], vl.T[64:]], axis=0)
-            gsend[slot] += dot6(lhs, vh, vm, vl, NN)
+            prod = dot6(lhs, vh, vm, vl, NN)
+            gacc[...] += prod
+
+        take(0)
+        parts(0)
+        more_loads(0)
+
+        def trip(j, _):
+            take(j)
+            gram(j - 1)
+            parts(j)
+            more_loads(j)
             return 0
-
-        lax.fori_loop(0, n, chunk, 0)
+        lax.fori_loop(1, n, trip, 0)
+        gram(n - 1)
+        gsend[slot, pl.ds(0, 192)] = gacc[:, pl.ds(0, 128)]
+        gsend[slot, pl.ds(192, 64)] = gacc[pl.ds(128, 64), pl.ds(128, 128)]
 
     def form_t(qn, slot):
         zero = jnp.zeros((64, 128), F32)
-        rows = []
-        for e in range(4):
-            dx = (e // 2 + xx) % 2
-            dk = (e % 2 + kk) % 2
-            val = tbv[dx * 2 + dk, qn]
+
+        def panel(e):
+            val = tbv[(e // 2 + xx) % 2 * 2 + (e % 2 + kk) % 2, qn]
             other = pltpu.roll(val, 64, 1)
-            if e % 2 == 0:
-                piece = jnp.where(left64, jnp.where(kk == 0, val, other), 0.0)
-            else:
-                piece = jnp.where(left64, 0.0, jnp.where(kk == 0, other, val))
-            rows.append(jnp.concatenate([piece, zero] if e < 2 else [zero, piece], axis=1))
-        s0 = jnp.concatenate(rows, axis=0)
-        gram = jnp.concatenate([jnp.zeros((64, 256), F32), gsend[slot] + grecv[slot]], axis=0)
-        bi = lax.broadcasted_iota(jnp.int32, (256, 256), 0) // 64
-        bj = lax.broadcasted_iota(jnp.int32, (256, 256), 1) // 64
-        near = ((bi == 1) & (bj == 0)) | ((bi == 3) & (bj == 2))
-        far = (bi >= 2) & (bj < 2)
-        for mask in (near, far):
-            gm = split3(jnp.where(mask, gram, 0.0))
-            sp = split3(s0)
-            st = jnp.concatenate(sp, axis=0)
-            mid = dot6(st, *gm, NN)
-            s0 = s0 - dot6(stack3(mid), *sp, NN)
-        ts[slot, kk] = s0
+            return (jnp.where(left64, jnp.where(kk == 0, val, other), 0.0),
+                    jnp.where(left64, 0.0, jnp.where(kk == 0, other, val)))
+
+        def padded(val):
+            return split3(jnp.concatenate([val, zero], axis=0))
+
+        gram = gsend[slot] + grecv[slot]
+        first, second = [], []
+        for pair in range(2):
+            low, high = panel(2 * pair)[0], panel(2 * pair + 1)
+            near = jnp.where(left64, gram[192 * pair:192 * pair + 64], 0.0)
+            first.append(dot6(stack3(high[0]), *padded(near), NN))
+            second.append((low, high[1]))
+        pairs = []
+        for pair in range(2):
+            low, high = second[pair]
+            pairs.append(jnp.concatenate([low, high - dot6(stack3(first[pair]), *padded(low), NN)], axis=0))
+        far = dot6(stack3(pairs[1]), *split3(gram[64:192]), NN)
+        far = dot6(stack3(far), *split3(pairs[0]), NN)
+        ts[slot, kk, pl.ds(0, 128), pl.ds(0, 128)] = pairs[0]
+        ts[slot, kk, pl.ds(0, 128), pl.ds(128, 128)] = jnp.zeros((128, 128), F32)
+        ts[slot, kk, pl.ds(128, 128), pl.ds(0, 128)] = -far
+        ts[slot, kk, pl.ds(128, 128), pl.ds(128, 128)] = pairs[1]
 
     def update(s, slot, par, ch):
         yst = ys[...]
@@ -235,6 +294,8 @@
         cols = pl.ds(pl.multiple_of((2 * s + yy) * 128, 128), 128)
         return (pltpu.make_async_copy(osb.at[s, ch, yy], o.at[rows, cols], o_l.at[s, ch]),
                 remote(osb.at[s, ch, 1 - yy], o.at[rows, cols], o_s.at[s, ch], o_r.at[s, ch], dev_y))
+
+    events = v_table()
 
     def step(g, _):
         i = g // 4 - 1
@@ -247,31 +308,19 @@
         nxt = (i + 1) % 2
         more = i < 15
 
-        @pl.when((sub == 0) & more)
-        def _():
-            at_q(qn, pass_on)
-
-            @pl.when(i + AHEAD < NBLK)
+        for quarter in range(4):
+            here = {trip: run_of(ev) for (trip, at), ev in events.items() if at == quarter}
+
+            @pl.when(sub == quarter)
             def _():
-                at_q(15 - (i + AHEAD), send_own)
-
-            @pl.when(qn % 2 == 1)
-            def _():
-                ch = qn // 2
-
-                @pl.when(ch >= 2)
-                def _():
-                    z_copy(ch - 2).start()
-                z_copy(ch).wait_recv()
-                for cp in z_loads(ch):
-                    cp.start()
+                at_trip(i, here)
 
         @pl.when(g == 0)
         def _():
             t_copy(0, 1).wait_recv()
             t_copy(0, 2).start()
 
-        @pl.when(g == 3)
+        @pl.when(g == 2)
         def _():
             t_copy(0, 0).wait_recv()
             t_copy(0, 2).wait_recv()
@@ -293,16 +342,19 @@
                 for piece, val in enumerate(split3(ts[cur, pp])):
                     tp[pp, piece] = val
 
-        @pl.when((sub == 1) & more)
-        def _():
-            at_q(qn, pass_diag)
+        @pl.when((sub == 0) & more)
+        def _():
+            prepare(qn, nxt)
+
+        @pl.when((sub == 1) & more & (qn % 2 == 1))
+        def _():
+            ch = qn // 2
+            z_copy(ch).wait_recv()
+            for cp in z_loads(ch):
+                cp.start()
 
         @pl.when((sub == 2) & more)
         def _():
-            at_q(qn, all_here)
-            prepare(qn, nxt)
-            g_copy(nxt).start()
-
             @pl.when(qn % 2 == 1)
             def _():
                 ch = qn // 2
@@ -312,8 +364,6 @@
                     for y1 in range(2):
                         xt[ss, ch, :, pl.ds(y1 * 256, 256)] = zst[ss, y1].T
 
-        @pl.when((sub == 3) & more)
-        def _():
             g_copy(nxt).wait()
             form_t(qn, nxt)
             s_copy(nxt).start()
@@ -331,6 +381,7 @@
             w_sum = wsend[s, par] + wrecv[s, par]
             y_val = dot6(stack3(w_sum), tp[par, 0], tp[par, 1], tp[par, 2], NN)
             ys[...] = stack3(y_val)
+            update(s, cur, par, 7)
 
         @pl.when(has_w)
         def _():
@@ -338,11 +389,9 @@
 
         @pl.when(has_u & has_w)
         def _():
-            update(s, cur, par, 7)
-
             def both(j, _):
+                project(s, w_slot, w_par, 8 - j, w_par)
                 update(s, cur, par, 7 - j)
-                project(s, w_slot, w_par, 8 - j, w_par)
                 return 0
             lax.fori_loop(1, n, both, 0)
 
@@ -354,17 +403,28 @@
             lax.fori_loop(jnp.where(has_u, n - 1, 0), n_w, rest, 0)
             w_copy(s, w_par).start()
 
+        @pl.when((sub == 0) & more)
+        def _():
+            g_copy(nxt).start()
+
+            @pl.when((qn % 2 == 1) & (qn >= 5))
+            def _():
+                z_copy(qn // 2 - 2).start()
+
         @pl.when(has_u & jnp.logical_not(has_w))
         def _():
-            def last(j, _):
-                ch = 7 - j
-                new = update(s, cur, par, ch)
+            def give(ch):
                 for y1 in range(2):
-                    osb[s, ch, y1] = new[:, y1 * 256:(y1 + 1) * 256].T
+                    osb[s, ch, y1] = xt[s, ch, :, pl.ds(y1 * 256, 256)].T
                 for cp in out_copies(s, ch):
                     cp.start()
+
+            def last(j, _):
+                give(8 - j)
+                update(s, cur, par, 7 - j)
                 return 0
-            lax.fori_loop(0, 8, last, 0)
+            lax.fori_loop(1, 8, last, 0)
+            give(0)
         return 0
 
     lax.fori_loop(0, 4 * (NBLK + 1), step, 0)
@@ -410,8 +470,9 @@
                 vmem((384, 256), BF16),
                 vmem((2, 2, 128, 256), F32),
                 vmem((2, 2, 128, 256), F32),
-                vmem((2, 192, 256), F32),
-                vmem((2, 192, 256), F32),
+                vmem((192, 256), F32),
+                vmem((2, 256, 128), F32),
+                vmem((2, 256, 128), F32),
                 vmem((2, 8, 2, 256, 128), F32),
                 dma((NBLK, 7)), dma((NBLK, 7)),
                 dma((8,)), dma((8,)), dma((2,)),

time: 640 us -> 485 us (0.76)
  Pallas kernels: 631 us -> 472 us
    pallas_call x1, Pallas kernels: 631 us -> 472 us  [local_apply(): pl.pallas_call(kernel, out_shape=(jax.ShapeDtypeStruct((2048, 512), F32),...]
where the time goes in v2:
time: 485 us; the launch traced here: 479 us
  Pallas kernels  472 us (97%)
  local copies, waits for them, and re-layouts  7.61 us (2%)
    pallas_call x1, Pallas kernels, local_apply(): pl.pallas_call(kernel, out_shape=(jax.ShapeDtypeStruct((2048, 512), F32),...  472 us

profile of v2, /device:TPU:0, one launch (start us, length us, event | category | flops | bytes accessed | tf_op | source)
XLA Modules:
  0.0 479.4 jit_solution(15779310764536087961)
XLA Ops:
  0.0 1.6 copy.4
  1.6 1.4 reshape.10.tt
  3.0 471.8 %shard_map.37 = (f32[2048,512]{1,0:T(8,128)}, f32[16,7,2048,128]{3,2,1,0:T(8,128)}, f32[2,2048,128]{2,1,0:T(8,128)}) custom-call(f32[2048,2048]{1,0:T(8,128)} %v.1, f32[16,64,128]{2,1,0:T(8,128)} %reshape.10.tt, f32[4,2048,128]{2,1,0:T(8,128)} %bitcast.6), custom_call_target="tpu_custom_call" | custom-call | tf_op jit(solution)/shard_map/pallas_call | solution.py:455
  474.8 4.6 copy.6

commit v3 on v2

--- a/solution.py
+++ b/solution.py
@@ -9,6 +9,10 @@
 BF16 = jnp.bfloat16
 MESH = pl.DeviceIdType.MESH
 NBLK = 16
+OWN = (None, None, None, 0, 3, 3, 13, 13, 3, 12, 24, 25, 34, 39, 44, 49)
+FWD = (None, 3, 3, 6, 11, 8, 19, 21, 19, 21, 31, 35, 39, 46, 49, 55)
+DIAG = (None, 3, 4, 10, 13, 14, 22, 25, 29, 32, 34, 41, 43, 49, 53, 57)
+HERE = (None, 3, 7, 11, 15, 19, 23, 27, 31, 35, 39, 43, 47, 51, 55, 59)
 NT = (((1,), (1,)), ((), ()))
 NN = (((1,), (0,)), ((), ()))
 
@@ -37,18 +41,13 @@
 def v_table():
     table = {}
 
-    def add(trip, quarter, what, blk):
-        if 0 <= blk < NBLK:
-            table.setdefault((trip, quarter), []).append((what, blk))
-
-    for trip in range(-1, NBLK):
-        if trip >= 0:
-            add(trip, 0, 'fwd', trip + 4)
-            add(trip, 2, 'diag', trip + 3)
-        add(trip, 0, 'own', trip + 6)
-        add(trip, 3, 'here', trip + 2)
-    for quarter, what, blk in ((1, 'fwd', 2), (1, 'diag', 1), (2, 'fwd', 3), (3, 'diag', 2)):
-        table.setdefault((-1, quarter), []).insert(0, (what, blk))
+    def add(at, what, blk):
+        table.setdefault((at // 4 - 1, at % 4), []).append((what, blk))
+
+    for what, quarters in (('fwd', FWD), ('own', OWN), ('diag', DIAG), ('here', HERE)):
+        for blk, at in enumerate(quarters):
+            if at is not None:
+                add(at, what, blk)
     return table
 
 
@@ -138,9 +137,9 @@
                 do[what](15 - blk)
         return run
 
-    def z_copy(ch):
-        rows = pl.ds(pl.multiple_of(256 * ch, 256), 256)
-        return remote(z4.at[pl.ds(2 * (1 - zz), 2), rows], zb.at[:, rows], z_s.at[ch], z_r.at[ch], dev_z)
+    def z_copy(ch, y1):
+        rows = pl.ds(mult(256 * ch, 256), 256)
+        return remote(z4.at[2 * (1 - zz) + y1, rows], zb.at[y1, rows], z_s.at[ch, y1], z_r.at[ch, y1], dev_z)
 
     def z_loads(ch):
         rows = pl.ds(pl.multiple_of(256 * ch, 256), 256)
@@ -168,19 +167,16 @@
     own_t = pltpu.make_async_copy(tt, tbv.at[0], tb_l)
     own_t.start()
     send_own(15)
-    send_own(14)
     for way in range(2):
         t_copy(0, way).start()
-    z_copy(7).start()
-    z_copy(6).start()
+    for y1 in range(2):
+        z_copy(7, y1).start()
+    pass_on(15)
+    for y1 in range(2):
+        z_copy(6, y1).start()
     send_own(13)
-    pass_on(15)
-    pass_on(14)
-    send_own(12)
     pass_diag(15)
-    send_own(11)
-    for way in range(2):
-        t_copy(1, way).start()
+    send_own(14)
     own_t.wait()
     all_here(15)
 
@@ -214,9 +210,8 @@
                         if h == 0:
                             a0 = jnp.where(empty, 0.0, a0)
                             a1 = jnp.where(empty, 0.0, a1)
-                        r0 = pltpu.roll(a0, 64, 1)
-                        r1 = pltpu.roll(a1, 64, 1)
-                        vals = (jnp.where(left, a0, r1), jnp.where(left, r0, a1))
+                        swap = pltpu.roll(jnp.where(left, a1, a0), 64, 1)
+                        vals = (jnp.where(left, a0, swap), jnp.where(left, swap, a1))
                         for par in range(2):
                             for piece, val in enumerate(split3(vals[par])):
                                 vp[slot, par, piece, ch, pl.ds(y1 * 256 + h * 128, 128),
@@ -286,8 +281,8 @@
         xt[s, ch] = new
         return new
 
-    def project(s, slot, par, ch, into):
-        wsend[s, into] += dot6(stack3(xt[s, ch]), vp[slot, par, 0, ch], vp[slot, par, 1, ch], vp[slot, par, 2, ch], NN)
+    def project(s, slot, par, ch):
+        return dot6(stack3(xt[s, ch]), vp[slot, par, 0, ch], vp[slot, par, 1, ch], vp[slot, par, 2, ch], NN)
 
     def out_copies(s, ch):
         rows = pl.ds(pl.multiple_of(256 * ch, 256), 256)
@@ -315,25 +310,34 @@
             def _():
                 at_trip(i, here)
 
-        @pl.when(g == 0)
+        @pl.when(g == 1)
         def _():
             t_copy(0, 1).wait_recv()
             t_copy(0, 2).start()
 
-        @pl.when(g == 2)
+        @pl.when(g == 3)
         def _():
             t_copy(0, 0).wait_recv()
             t_copy(0, 2).wait_recv()
 
-        @pl.when(g == 5)
+        @pl.when(g == 6)
+        def _():
+            t_copy(1, 0).start()
+            t_copy(1, 1).start()
+
+        @pl.when(g == 12)
         def _():
             t_copy(1, 1).wait_recv()
             t_copy(1, 2).start()
 
-        @pl.when(g == 9)
+        @pl.when(g == 15)
         def _():
             t_copy(1, 0).wait_recv()
             t_copy(1, 2).wait_recv()
+
+        @pl.when((sub == 0) & more)
+        def _():
+            prepare(qn, nxt)
 
         @pl.when((sub == 0) & (i >= 0))
         def _():
@@ -342,28 +346,25 @@
                 for piece, val in enumerate(split3(ts[cur, pp])):
                     tp[pp, piece] = val
 
-        @pl.when((sub == 0) & more)
-        def _():
-            prepare(qn, nxt)
-
         @pl.when((sub == 1) & more & (qn % 2 == 1))
         def _():
             ch = qn // 2
-            z_copy(ch).wait_recv()
+            for y1 in range(2):
+                z_copy(ch, y1).wait_recv()
             for cp in z_loads(ch):
                 cp.start()
 
-        @pl.when((sub == 2) & more)
-        def _():
-            @pl.when(qn % 2 == 1)
-            def _():
-                ch = qn // 2
-                for cp in z_loads(ch):
-                    cp.wait()
-                for ss in range(2):
-                    for y1 in range(2):
-                        xt[ss, ch, :, pl.ds(y1 * 256, 256)] = zst[ss, y1].T
-
+        @pl.when((sub == 2) & more & (qn % 2 == 1))
+        def _():
+            ch = qn // 2
+            for cp in z_loads(ch):
+                cp.wait()
+            for ss in range(2):
+                for y1 in range(2):
+                    xt[ss, ch, :, pl.ds(y1 * 256, 256)] = zst[ss, y1].T
+
+        @pl.when((sub == 3) & more)
+        def _():
             g_copy(nxt).wait()
             form_t(qn, nxt)
             s_copy(nxt).start()
@@ -375,44 +376,49 @@
         w_slot = jnp.where(sub < 2, cur, nxt)
         n_w = jnp.where(sub < 2, n, 8 - qn // 2)
 
-        @pl.when(has_u)
-        def _():
+        def solve():
             w_copy(s, par).wait()
             w_sum = wsend[s, par] + wrecv[s, par]
-            y_val = dot6(stack3(w_sum), tp[par, 0], tp[par, 1], tp[par, 2], NN)
-            ys[...] = stack3(y_val)
+            ys[...] = stack3(dot6(stack3(w_sum), tp[par, 0], tp[par, 1], tp[par, 2], NN))
+
+        for chunks in range(1, 9):
+            @pl.when(has_u & has_w & (n == chunks))
+            def _():
+                solve()
+                total = None
+                for j in range(chunks + 1):
+                    if j < chunks:
+                        update(s, cur, par, 7 - j)
+                    if j > 0:
+                        prod = project(s, w_slot, w_par, 8 - j)
+                        total = prod if total is None else total + prod
+                wsend[s, w_par] = total
+
+        @pl.when(has_w & jnp.logical_not(has_u))
+        def _():
+            wsend[s, w_par] = project(s, w_slot, w_par, 7)
+
+        @pl.when(has_w & has_u & (n_w > n))
+        def _():
+            wsend[s, w_par] += project(s, w_slot, w_par, 7 - n)
+
+        @pl.when(has_w)
+        def _():
+            w_copy(s, w_par).start()
+
+        @pl.when((sub == 0) & more)
+        def _():
+            g_copy(nxt).start()
+
+        @pl.when(((sub == 1) | (sub == 2)) & (qn % 2 == 1) & (qn >= 5))
+        def _():
+            z_copy(qn // 2 - 2, sub - 1).start()
+
+        @pl.when(has_u & jnp.logical_not(has_w))
+        def _():
+            solve()
             update(s, cur, par, 7)
 
-        @pl.when(has_w)
-        def _():
-            wsend[s, w_par] = jnp.zeros((128, 256), F32)
-
-        @pl.when(has_u & has_w)
-        def _():
-            def both(j, _):
-                project(s, w_slot, w_par, 8 - j, w_par)
-                update(s, cur, par, 7 - j)
-                return 0
-            lax.fori_loop(1, n, both, 0)
-
-        @pl.when(has_w)
-        def _():
-            def rest(j, _):
-                project(s, w_slot, w_par, 7 - j, w_par)
-                return 0
-            lax.fori_loop(jnp.where(has_u, n - 1, 0), n_w, rest, 0)
-            w_copy(s, w_par).start()
-
-        @pl.when((sub == 0) & more)
-        def _():
-            g_copy(nxt).start()
-
-            @pl.when((qn % 2 == 1) & (qn >= 5))
-            def _():
-                z_copy(qn // 2 - 2).start()
-
-        @pl.when(has_u & jnp.logical_not(has_w))
-        def _():
             def give(ch):
                 for y1 in range(2):
                     osb[s, ch, y1] = xt[s, ch, :, pl.ds(y1 * 256, 256)].T
@@ -437,7 +443,8 @@
             slab(qq, idx).wait_send()
 
     def drain(ch, _):
-        z_copy(ch).wait_send()
+        for y1 in range(2):
+            z_copy(ch, y1).wait_send()
         for s in range(2):
             local, far = out_copies(s, ch)
             local.wait()
@@ -475,7 +482,7 @@
                 vmem((2, 256, 128), F32),
                 vmem((2, 8, 2, 256, 128), F32),
                 dma((NBLK, 7)), dma((NBLK, 7)),
-                dma((8,)), dma((8,)), dma((2,)),
+                dma((8, 2)), dma((8, 2)), dma((2,)),
                 dma((2, 3)), dma((2, 3)), dma,
                 dma((2,)), dma((2,)),
                 dma((2, 2)), dma((2, 2)),

time: 485 us -> 420 us (0.87)
  Pallas kernels: 472 us -> 409 us
    pallas_call x1, Pallas kernels: 472 us -> 409 us  [local_apply(): pl.pallas_call(kernel, out_shape=(jax.ShapeDtypeStruct((2048, 512), F32),...]
where the time goes in v3:
time: 420 us; the launch traced here: 417 us
  Pallas kernels  409 us (97%)
  local copies, waits for them, and re-layouts  7.61 us (2%)
    pallas_call x1, Pallas kernels, local_apply(): pl.pallas_call(kernel, out_shape=(jax.ShapeDtypeStruct((2048, 512), F32),...  409 us

profile of v3, /device:TPU:0, one launch (start us, length us, event | category | flops | bytes accessed | tf_op | source)
XLA Modules:
  0.0 417.1 jit_solution(18388136834484214527)
XLA Ops:
  0.0 1.6 copy.4
  1.6 1.4 reshape.10.tt
  3.0 409.5 %shard_map.37 = (f32[2048,512]{1,0:T(8,128)}, f32[16,7,2048,128]{3,2,1,0:T(8,128)}, f32[2,2048,128]{2,1,0:T(8,128)}) custom-call(f32[2048,2048]{1,0:T(8,128)} %v.1, f32[16,64,128]{2,1,0:T(8,128)} %reshape.10.tt, f32[4,2048,128]{2,1,0:T(8,128)} %bitcast.6), custom_call_target="tpu_custom_call" | custom-call | tf_op jit(solution)/shard_map/pallas_call | solution.py:462
  412.5 4.6 %copy.6 = f32[2048,512]{1,0:T(8,128)} copy(f32[2048,512]{1,0:T(8,128)} %get-tuple-element.6) | data formatting | bytes 8388608

commit v4 on v3

--- a/solution.py
+++ b/solution.py
@@ -9,10 +9,11 @@
 BF16 = jnp.bfloat16
 MESH = pl.DeviceIdType.MESH
 NBLK = 16
-OWN = (None, None, None, 0, 3, 3, 13, 13, 3, 12, 24, 25, 34, 39, 44, 49)
-FWD = (None, 3, 3, 6, 11, 8, 19, 21, 19, 21, 31, 35, 39, 46, 49, 55)
-DIAG = (None, 3, 4, 10, 13, 14, 22, 25, 29, 32, 34, 41, 43, 49, 53, 57)
-HERE = (None, 3, 7, 11, 15, 19, 23, 27, 31, 35, 39, 43, 47, 51, 55, 59)
+REST = 0
+OWN = (None, None, None, 4, 0, 4, 6, 9, 11, 20, 21, 21, 35, 36, 44, 51)
+FWD = (None, 0, 3, 6, 6, 8, 19, 15, 17, 26, 32, 31, 40, 47, 49, 56)
+DIAG = (None, 0, 4, 9, 9, 17, 23, 27, 29, 32, 36, 40, 46, 50, 53, 58)
+HERE = (None, 3, 8, 11, 15, 19, 24, 28, 32, 36, 39, 43, 48, 51, 55, 59)
 NT = (((1,), (1,)), ((), ()))
 NN = (((1,), (0,)), ((), ()))
 
@@ -51,8 +52,8 @@
     return table
 
 
-def kernel(v, tt, z4, o, vb, zb, vp, xt, stage, zst, tbv, ts, tp, ys, wsend, wrecv, gacc, gsend, grecv, osb,
-           v_s, v_r, z_s, z_r, zl, tb_s, tb_r, tb_l, t_s, t_r, w_s, w_r, g_s, g_r, st_a, st_b, o_s, o_r, o_l):
+def kernel(v, tt, z4, o, vb, zb, vp, xt, stage, zst, traw, tbv, ts, tp, ys, whalf, wsend, wrecv, gacc, gsend, grecv, osb, early, landed, y_out, y_in, yin,
+           v_s, v_r, z_s, z_r, zl, tb_s, tb_r, tb_l, t_s, t_r, w_s, w_r, g_s, g_r, st_a, st_b, o_s, o_r, e_s, e_r, y_s, y_r):
     r = lax.axis_index('row')
     c = lax.axis_index('col')
     zz, yy, xx, kk = r // 2, r % 2, c // 2, c % 2
@@ -125,7 +126,7 @@
     def all_here(qq):
         for idx in (0, 2, 4, 6):
             slab(qq, idx).wait_recv()
-        for j in range(min(2, 8 - qq // 2)):
+        for j in range(min(4, 8 - qq // 2)):
             for cp in stage_loads(qq, 7 - j, j):
                 cp.start()
 
@@ -146,12 +147,12 @@
         return (pltpu.make_async_copy(z4.at[pl.ds(2 * zz, 2), rows], zst.at[zz], zl.at[0]),
                 pltpu.make_async_copy(zb.at[:, rows], zst.at[1 - zz], zl.at[1]))
 
-    halves = ((12, 4), (0, 12))
+    t_parts = ((12, 4), (0, 12))
 
     def t_copy(half, way):
-        q0, nq = halves[half]
+        q0, nq = t_parts[half]
         part = pl.ds(q0, nq)
-        src = tbv.at[2, part] if way == 2 else tt.at[part]
+        src = tbv.at[2, part] if way == 2 else tbv.at[0, part]
         return remote(src, tbv.at[way + 1, part], tb_s.at[half, way], tb_r.at[half, way],
                       dev_x if way == 1 else dev_p)
 
@@ -164,20 +165,25 @@
     def s_copy(slot):
         return remote(ts.at[slot, kk], ts.at[slot, kk], t_s.at[slot], t_r.at[slot], dev_p)
 
-    own_t = pltpu.make_async_copy(tt, tbv.at[0], tb_l)
+    own_t = pltpu.make_async_copy(tt, traw, tb_l)
     own_t.start()
     send_own(15)
-    for way in range(2):
-        t_copy(0, way).start()
+    own_t.wait()
+
+    def pack(q, _):
+        tbv[0, q] = jnp.concatenate([traw[2 * q], traw[2 * q + 1]], axis=0).T
+        return 0
+    lax.fori_loop(0, NBLK, pack, 0)
+    for y1 in range(2):
+        z_copy(6, y1).start()
+    send_own(14)
     for y1 in range(2):
         z_copy(7, y1).start()
     pass_on(15)
-    for y1 in range(2):
-        z_copy(6, y1).start()
     send_own(13)
     pass_diag(15)
-    send_own(14)
-    own_t.wait()
+    for way in range(2):
+        t_copy(0, way).start()
     all_here(15)
 
     lane = lax.broadcasted_iota(jnp.int32, (128, 128), 1)
@@ -191,13 +197,13 @@
 
         def take(j):
             ch = 7 - j
-            buf = j % 2
+            buf = j % 4
             for cp in stage_loads(qn, ch, buf):
                 cp.wait()
 
         def parts(j):
             ch = 7 - j
-            buf = j % 2
+            buf = j % 4
             empty = (qn % 2 == 1) & (ch == cq)
             for y1 in range(2):
                 dy = (y1 + yy) % 2
@@ -218,9 +224,9 @@
                                    pl.ds(pair * 128, 128)] = val
 
         def more_loads(j):
-            @pl.when(j + 2 < n)
+            @pl.when(j + 4 < n)
             def _():
-                for cp in stage_loads(qn, 5 - j, j % 2):
+                for cp in stage_loads(qn, 3 - j, j % 4):
                     cp.start()
 
         def gram(j):
@@ -241,8 +247,9 @@
             return 0
         lax.fori_loop(1, n, trip, 0)
         gram(n - 1)
-        gsend[slot, pl.ds(0, 192)] = gacc[:, pl.ds(0, 128)]
-        gsend[slot, pl.ds(192, 64)] = gacc[pl.ds(128, 64), pl.ds(128, 128)]
+        gsend[slot, pl.ds(0, 64)] = jnp.where(left64, gacc[pl.ds(0, 64), pl.ds(0, 128)],
+                                              pltpu.roll(gacc[pl.ds(128, 64), pl.ds(128, 128)], 64, 1))
+        gsend[slot, pl.ds(64, 128)] = gacc[pl.ds(64, 128), pl.ds(0, 128)]
 
     def form_t(qn, slot):
         zero = jnp.zeros((64, 128), F32)
@@ -260,7 +267,8 @@
         first, second = [], []
         for pair in range(2):
             low, high = panel(2 * pair)[0], panel(2 * pair + 1)
-            near = jnp.where(left64, gram[192 * pair:192 * pair + 64], 0.0)
+            near = gram[:64] if pair == 0 else pltpu.roll(gram[:64], 64, 1)
+            near = jnp.where(left64, near, 0.0)
             first.append(dot6(stack3(high[0]), *padded(near), NN))
             second.append((low, high[1]))
         pairs = []
@@ -281,14 +289,33 @@
         xt[s, ch] = new
         return new
 
+    def project_half(s, slot, par, ch, t):
+        part = pl.ds(256 * t, 256)
+        return dot6(stack3(xt[s, ch, :, part]), *(vp[slot, par, piece, ch, part] for piece in range(3)), NN)
+
     def project(s, slot, par, ch):
         return dot6(stack3(xt[s, ch]), vp[slot, par, 0, ch], vp[slot, par, 1, ch], vp[slot, par, 2, ch], NN)
 
-    def out_copies(s, ch):
-        rows = pl.ds(pl.multiple_of(256 * ch, 256), 256)
-        cols = pl.ds(pl.multiple_of((2 * s + yy) * 128, 128), 128)
-        return (pltpu.make_async_copy(osb.at[s, ch, yy], o.at[rows, cols], o_l.at[s, ch]),
-                remote(osb.at[s, ch, 1 - yy], o.at[rows, cols], o_s.at[s, ch], o_r.at[s, ch], dev_y))
+    near_half = pl.ds(pl.multiple_of(yy * 256, 256), 256)
+    far_half = pl.ds(pl.multiple_of((1 - yy) * 256, 256), 256)
+
+    def mult_rows(ch):
+        return pl.ds(mult(256 * ch, 256), 256)
+
+    def own_cols(s):
+        return pl.ds(pl.multiple_of((2 * s + yy) * 128, 128), 128)
+
+    def far_cols(s):
+        return pl.ds(pl.multiple_of((2 * s + 1 - yy) * 128, 128), 128)
+
+    def out_copy(ch):
+        return remote(osb.at[ch], o.at[mult_rows(ch), own_cols(0)], o_s.at[ch], o_r.at[ch], dev_y)
+
+    def early_copy():
+        return remote(early, landed, e_s, e_r, dev_y)
+
+    def y_copy(at):
+        return remote(y_out.at[at], y_in.at[at], y_s.at[at], y_r.at[at], dev_y)
 
     events = v_table()
 
@@ -320,17 +347,17 @@
             t_copy(0, 0).wait_recv()
             t_copy(0, 2).wait_recv()
 
-        @pl.when(g == 6)
+        @pl.when(g == REST)
         def _():
             t_copy(1, 0).start()
             t_copy(1, 1).start()
 
-        @pl.when(g == 12)
+        @pl.when(g == REST + 6)
         def _():
             t_copy(1, 1).wait_recv()
             t_copy(1, 2).start()
 
-        @pl.when(g == 15)
+        @pl.when(g == REST + 9)
         def _():
             t_copy(1, 0).wait_recv()
             t_copy(1, 2).wait_recv()
@@ -376,23 +403,36 @@
         w_slot = jnp.where(sub < 2, cur, nxt)
         n_w = jnp.where(sub < 2, n, 8 - qn // 2)
 
+        tell = (i >= NBLK - 2) & (s == 1)
+        y_at = jnp.where(tell, 2 * (i - (NBLK - 2)) + 1 - par, 4)
+
         def solve():
             w_copy(s, par).wait()
             w_sum = wsend[s, par] + wrecv[s, par]
-            ys[...] = stack3(dot6(stack3(w_sum), tp[par, 0], tp[par, 1], tp[par, 2], NN))
+            halves = [dot6(stack3(w_sum[64 * h:64 * h + 64]), tp[par, 0], tp[par, 1], tp[par, 2], NN)
+                      for h in range(2)]
+            y_val = jnp.concatenate(halves, axis=0)
+            ys[...] = stack3(y_val)
+            y_out[y_at] = y_val
 
         for chunks in range(1, 9):
             @pl.when(has_u & has_w & (n == chunks))
             def _():
                 solve()
-                total = None
+                totals = [None, None]
                 for j in range(chunks + 1):
                     if j < chunks:
                         update(s, cur, par, 7 - j)
                     if j > 0:
-                        prod = project(s, w_slot, w_par, 8 - j)
-                        total = prod if total is None else total + prod
-                wsend[s, w_par] = total
+                        for t in range(2):
+                            prod = project_half(s, w_slot, w_par, 8 - j, t)
+                            totals[t] = prod if totals[t] is None else totals[t] + prod
+                wsend[s, w_par] = totals[0]
+                whalf[...] = totals[1]
+
+        @pl.when(has_u & has_w)
+        def _():
+            wsend[s, w_par] += whalf[...]
 
         @pl.when(has_w & jnp.logical_not(has_u))
         def _():
@@ -414,23 +454,62 @@
         def _():
             z_copy(qn // 2 - 2, sub - 1).start()
 
-        @pl.when(has_u & jnp.logical_not(has_w))
+        @pl.when(tell & has_w)
+        def _():
+            y_copy(y_at).start()
+
+        @pl.when((i == NBLK - 3) & (sub == 3))
+        def _():
+            def keep(ch, _):
+                early[ch] = xt[1, ch, :, far_half]
+                return 0
+            lax.fori_loop(0, 8, keep, 0)
+            early_copy().start()
+
+        @pl.when((i == NBLK - 1) & (sub == 2))
         def _():
             solve()
-            update(s, cur, par, 7)
+            update(0, cur, 0, 7)
 
             def give(ch):
-                for y1 in range(2):
-                    osb[s, ch, y1] = xt[s, ch, :, pl.ds(y1 * 256, 256)].T
-                for cp in out_copies(s, ch):
-                    cp.start()
+                osb[ch] = xt[0, ch, :, far_half].T
+                out_copy(ch).start()
+                o[mult_rows(ch), own_cols(0)] = xt[0, ch, :, near_half].T
 
             def last(j, _):
                 give(8 - j)
-                update(s, cur, par, 7 - j)
+                update(0, cur, 0, 7 - j)
                 return 0
             lax.fori_loop(1, 8, last, 0)
             give(0)
+
+        @pl.when((i == NBLK - 1) & (sub == 3))
+        def _():
+            solve()
+            y_copy(3).start()
+
+            def near(pair, _):
+                yst = ys[...]
+                for ch in (2 * pair, 2 * pair + 1):
+                    delta = dot6(yst, *(vp[cur, 0, piece, ch, near_half] for piece in range(3)), NT)
+                    o[mult_rows(ch), own_cols(1)] = (xt[1, ch, :, near_half] - delta).T
+                return 0
+            lax.fori_loop(0, 4, near, 0)
+
+            early_copy().wait_recv()
+            for at in range(4):
+                y_copy(at).wait_recv()
+                yin[at] = stack3(y_in[at])
+
+            def far(pair, _):
+                for ch in (2 * pair, 2 * pair + 1):
+                    total = None
+                    for at in range(4):
+                        part = dot6(yin[at], *(vp[at // 2, 1 - at % 2, piece, ch, near_half] for piece in range(3)), NT)
+                        total = part if total is None else total + part
+                    o[mult_rows(ch), far_cols(1)] = (landed[ch] - total).T
+                return 0
+            lax.fori_loop(0, 4, far, 0)
         return 0
 
     lax.fori_loop(0, 4 * (NBLK + 1), step, 0)
@@ -442,56 +521,64 @@
         for idx in range(7):
             slab(qq, idx).wait_send()
 
+    early_copy().wait_send()
+    for at in range(4):
+        y_copy(at).wait_send()
+
     def drain(ch, _):
         for y1 in range(2):
             z_copy(ch, y1).wait_send()
-        for s in range(2):
-            local, far = out_copies(s, ch)
-            local.wait()
-            far.wait()
+        out_copy(ch).wait()
         return 0
     lax.fori_loop(0, 8, drain, 0)
 
 
 def solution(mesh):
     def local_apply(v_loc, t_loc, z_loc):
-        tt = jnp.swapaxes(t_loc, 1, 2).reshape(NBLK, 2, 64, 64).transpose(0, 2, 1, 3).reshape(NBLK, 64, 128)
         z4 = z_loc.reshape(4, 2048, 128)
         any_spec = pl.BlockSpec(memory_space=pl.ANY)
         dma, vmem = pltpu.SemaphoreType.DMA, pltpu.VMEM
         out = pl.pallas_call(
             kernel,
-            out_shape=(jax.ShapeDtypeStruct((2048, 512), F32),
+            out_shape=(pltpu.VMEM((2048, 512), F32),
                        jax.ShapeDtypeStruct((NBLK, 7, 2048, 128), F32),
                        jax.ShapeDtypeStruct((2, 2048, 128), F32)),
             in_specs=[any_spec] * 3,
-            out_specs=(any_spec,) * 3,
+            out_specs=(pl.BlockSpec(memory_space=pltpu.VMEM), any_spec, any_spec),
             scratch_shapes=[
                 vmem((2, 2, 3, 8, 512, 256), BF16),
                 vmem((2, 8, 128, 512), F32),
-                vmem((2, 8, 256, 128), F32),
+                vmem((4, 8, 256, 128), F32),
                 vmem((2, 2, 256, 128), F32),
+                vmem((32, 64, 64), F32),
                 vmem((4, NBLK, 64, 128), F32),
                 vmem((2, 2, 256, 256), F32),
                 vmem((2, 3, 256, 256), BF16),
                 vmem((384, 256), BF16),
+                vmem((128, 256), F32),
                 vmem((2, 2, 128, 256), F32),
                 vmem((2, 2, 128, 256), F32),
                 vmem((192, 256), F32),
-                vmem((2, 256, 128), F32),
-                vmem((2, 256, 128), F32),
-                vmem((2, 8, 2, 256, 128), F32),
+                vmem((2, 192, 128), F32),
+                vmem((2, 192, 128), F32),
+                vmem((8, 256, 128), F32),
+                vmem((8, 128, 256), F32),
+                vmem((8, 128, 256), F32),
+                vmem((5, 128, 256), F32),
+                vmem((4, 128, 256), F32),
+                vmem((4, 384, 256), BF16),
                 dma((NBLK, 7)), dma((NBLK, 7)),
                 dma((8, 2)), dma((8, 2)), dma((2,)),
                 dma((2, 3)), dma((2, 3)), dma,
                 dma((2,)), dma((2,)),
                 dma((2, 2)), dma((2, 2)),
                 dma((2,)), dma((2,)),
-                dma((2,)), dma((2,)),
-                dma((2, 8)), dma((2, 8)), dma((2, 8)),
+                dma((4,)), dma((4,)),
+                dma((8,)), dma((8,)),
+                dma, dma, dma((4,)), dma((4,)),
             ],
-            compiler_params=pltpu.CompilerParams(collective_id=0, has_side_effects=True, vmem_limit_bytes=64_000_000),
-        )(v_loc, tt, z4)
+            compiler_params=pltpu.CompilerParams(collective_id=0, has_side_effects=True, vmem_limit_bytes=56_000_000),
+        )(v_loc, t_loc, z4)
         return out[0]
 
     return jax.shard_map(local_apply, mesh=mesh,

time: 420 us -> 387 us (0.921)
  Pallas kernels: 409 us -> 384 us
  local copies, waits for them, and re-layouts: 7.61 us -> 2.02 us
    pallas_call x1, Pallas kernels: 409 us -> 384 us  [local_apply(): pl.pallas_call(kernel, out_shape=(pltpu.VMEM((2048, 512), F32), jax.Shape...]
where the time goes in v4:
time: 387 us; the launch traced here: 386 us
  Pallas kernels  384 us (99%)
    pallas_call x1, Pallas kernels, local_apply(): pl.pallas_call(kernel, out_shape=(pltpu.VMEM((2048, 512), F32), jax.Shape...  384 us

profile of v4, /device:TPU:0, one launch (start us, length us, event | category | flops | bytes accessed | tf_op | source)
XLA Modules:
  0.0 385.9 jit_solution(13884336734307669121)
XLA Ops:
  0.0 383.8 %shard_map.37 = (f32[2048,512]{1,0:T(8,128)S(1)}, f32[16,7,2048,128]{3,2,1,0:T(8,128)}, f32[2,2048,128]{2,1,0:T(8,128)}) custom-call(f32[2048,2048]{1,0:T(8,128)} %v.1, f32[32,64,64]{2,1,0:T(8,128)} %tt.1, f32[4,2048,128]{2,1,0:T(8,128)} %bitcast.1), custom_call_target="tpu_custom_call" | custom-call | tf_op jit(solution)/shard_map/pallas_call | solution.py:541
  383.8 2.0 copy.5

commit v5 on v4

--- a/solution.py
+++ b/solution.py
@@ -52,7 +52,7 @@
     return table
 
 
-def kernel(v, tt, z4, o, vb, zb, vp, xt, stage, zst, traw, tbv, ts, tp, ys, whalf, wsend, wrecv, gacc, gsend, grecv, osb, early, landed, y_out, y_in, yin,
+def kernel(v, tt, z4, o, vb, zb, vp, xt, stage, zst, traw, tbp, tbv, ts, tp, ys, whalf, wsend, wrecv, gacc, gsend, grecv, osb, early, landed, y_out, y_in, yin,
            v_s, v_r, z_s, z_r, zl, tb_s, tb_r, tb_l, t_s, t_r, w_s, w_r, g_s, g_r, st_a, st_b, o_s, o_r, e_s, e_r, y_s, y_r):
     r = lax.axis_index('row')
     c = lax.axis_index('col')
@@ -75,22 +75,33 @@
     def mult(val, by):
         return val if isinstance(val, int) else pl.multiple_of(val, by)
 
-    def own(qq, idx, dev):
-        r0 = 128 * qq
-        return remote(v.at[pl.ds(r0, 2048 - r0), pl.ds(r0, 128)], vb.at[qq, idx, pl.ds(r0, 2048 - r0)],
-                      v_s.at[qq, idx], v_r.at[qq, idx], dev)
-
-    def fwd(qq, src, idx, dev):
-        r0 = 128 * qq
-        return remote(vb.at[qq, src, pl.ds(r0, 2048 - r0)], vb.at[qq, idx, pl.ds(r0, 2048 - r0)],
-                      v_s.at[qq, idx], v_r.at[qq, idx], dev)
-
-    def slab(qq, idx):
+    def is_short(dy, dx, dk):
+        return 2 * zz + (yy + dy) % 2 < (xx + dx) % 2 * 2 + (kk + dk) % 2
+
+    sent = [is_short(*at) for at in ((0, 0, 0), (0, 0, 0), (0, 1, 0), (0, 0, 0), (1, 0, 0), (kk, 1 - kk, 0), (1, 1, 0))]
+    got = [is_short(*at) for at in ((0, 0, 1), (0, 1, 0), (0, 1, 1), (1, 0, 0), (1, 0, 1), (1, 1, 0), (1, 1, 1))]
+
+    def slab(qq, idx, short):
+        r0 = 128 * qq + (64 if short else 0)
+        rows = pl.ds(r0, 2048 - r0)
+        dev = {1: dev_x, 3: dev_y, 5: dev_d}.get(idx, dev_p)
         if idx in (0, 1, 3):
-            return own(qq, idx, {0: dev_p, 1: dev_x, 3: dev_y}[idx])
-        if idx == 5:
-            return fwd(qq, 1 + 2 * kk, 5, dev_d)
-        return fwd(qq, idx - 1, idx, dev_p)
+            src = v.at[rows, pl.ds(128 * qq, 128)]
+        else:
+            src = vb.at[qq, 1 + 2 * kk if idx == 5 else idx - 1, rows]
+        return remote(src, vb.at[qq, idx, rows], v_s.at[qq, idx], v_r.at[qq, idx], dev)
+
+    def send(qq, idx):
+        for short in (True, False):
+            @pl.when(sent[idx] == short)
+            def _():
+                slab(qq, idx, short).start()
+
+    def receive(qq, idx):
+        for short in (True, False):
+            @pl.when(got[idx] == short)
+            def _():
+                slab(qq, idx, short).wait_recv()
 
     def at_trip(i, table):
         for first in range(-1, NBLK, 4):
@@ -105,17 +116,17 @@
 
     def send_own(qq):
         for idx in (1, 3, 0):
-            slab(qq, idx).start()
+            send(qq, idx)
 
     def pass_on(qq):
         for idx in (1, 3):
-            slab(qq, idx).wait_recv()
+            receive(qq, idx)
         for idx in (5, 2, 4):
-            slab(qq, idx).start()
+            send(qq, idx)
 
     def pass_diag(qq):
-        slab(qq, 5).wait_recv()
-        slab(qq, 6).start()
+        receive(qq, 5)
+        send(qq, 6)
 
     def stage_loads(q, ch, buf):
         rows = pl.ds(mult(256 * ch, 256), 256)
@@ -125,7 +136,7 @@
 
     def all_here(qq):
         for idx in (0, 2, 4, 6):
-            slab(qq, idx).wait_recv()
+            receive(qq, idx)
         for j in range(min(4, 8 - qq // 2)):
             for cp in stage_loads(qq, 7 - j, j):
                 cp.start()
@@ -147,13 +158,13 @@
         return (pltpu.make_async_copy(z4.at[pl.ds(2 * zz, 2), rows], zst.at[zz], zl.at[0]),
                 pltpu.make_async_copy(zb.at[:, rows], zst.at[1 - zz], zl.at[1]))
 
-    t_parts = ((12, 4), (0, 12))
+    t_parts = ((6, 2), (0, 6))
 
     def t_copy(half, way):
         q0, nq = t_parts[half]
         part = pl.ds(q0, nq)
-        src = tbv.at[2, part] if way == 2 else tbv.at[0, part]
-        return remote(src, tbv.at[way + 1, part], tb_s.at[half, way], tb_r.at[half, way],
+        src = tbp.at[2, part] if way == 2 else tbp.at[0, part]
+        return remote(src, tbp.at[way + 1, part], tb_s.at[half, way], tb_r.at[half, way],
                       dev_x if way == 1 else dev_p)
 
     def w_copy(s, par):
@@ -170,10 +181,31 @@
     send_own(15)
     own_t.wait()
 
-    def pack(q, _):
-        tbv[0, q] = jnp.concatenate([traw[2 * q], traw[2 * q + 1]], axis=0).T
+    row64 = lax.broadcasted_iota(jnp.int32, (64, 128), 0)
+    lane64 = lax.broadcasted_iota(jnp.int32, (64, 128), 1)
+
+    def pack(pair, _):
+        low = jnp.concatenate([traw[4 * pair], traw[4 * pair + 2]], axis=0).T
+        high = jnp.concatenate([traw[4 * pair + 1].T, traw[4 * pair + 3].T], axis=0).T
+        col = lane64 % 64
+        tbp[0, pair, pl.ds(0, 64)] = jnp.where(row64 >= col, low, high)
+        diag = jnp.sum(jnp.where(row64 == col, high, 0.0), axis=0, keepdims=True)
+        tbp[0, pair, pl.ds(64, 8)] = jnp.broadcast_to(diag, (8, 128))
         return 0
-    lax.fori_loop(0, NBLK, pack, 0)
+
+    def unpack(at, _):
+        q, src = at // 4, at % 4
+        both = tbp[src, q // 2]
+        both = jnp.where(q % 2 == 1, pltpu.roll(both, 64, 1), both)
+        square, diag = both[:64], both[64:65]
+        even = jnp.where((lane64 < 64) & (row64 >= lane64), square, 0.0)
+        odd = jnp.where(row64 < lane64, square, jnp.where(row64 == lane64, jnp.broadcast_to(diag, (64, 128)), 0.0))
+        odd = jnp.where(lane64 < 64, odd, 0.0)
+        odd = jnp.concatenate([odd, jnp.zeros((64, 128), F32)], axis=0).T[:64]
+        tbv[src, q] = jnp.where(kk == 0, even, odd)
+        return 0
+
+    lax.fori_loop(0, NBLK // 2, pack, 0)
     for y1 in range(2):
         z_copy(6, y1).start()
     send_own(14)
@@ -190,6 +222,9 @@
     left = lane < 64
     left64 = left[:64]
 
+    def part_of(slot, par, piece, ch, rows=slice(None)):
+        return jnp.concatenate([vp[slot, par, piece, ch, side, rows] for side in range(2)], axis=1)
+
     def prepare(qn, slot):
         cq = qn // 2
         n = 8 - cq
@@ -201,10 +236,19 @@
             for cp in stage_loads(qn, ch, buf):
                 cp.wait()
 
+            @pl.when(j == n - 1)
+            def _():
+                @pl.when(qn % 2 == 1)
+                def _():
+                    stage[buf, :, pl.ds(0, 128)] = jnp.zeros((8, 128, 128), F32)
+                for rel in range(8):
+                    @pl.when(is_short(rel // 4, rel // 2 % 2, rel % 2))
+                    def _():
+                        stage[buf, rel, pl.ds(pl.multiple_of(128 * (qn % 2), 128), 64)] = jnp.zeros((64, 128), F32)
+
         def parts(j):
             ch = 7 - j
             buf = j % 4
-            empty = (qn % 2 == 1) & (ch == cq)
             for y1 in range(2):
                 dy = (y1 + yy) % 2
                 for h in range(2):
@@ -213,15 +257,11 @@
                         rel = dy * 4 + dx * 2
                         a0 = stage[buf, rel + kk, pl.ds(128 * h, 128), :]
                         a1 = stage[buf, rel + 1 - kk, pl.ds(128 * h, 128), :]
-                        if h == 0:
-                            a0 = jnp.where(empty, 0.0, a0)
-                            a1 = jnp.where(empty, 0.0, a1)
                         swap = pltpu.roll(jnp.where(left, a1, a0), 64, 1)
                         vals = (jnp.where(left, a0, swap), jnp.where(left, swap, a1))
                         for par in range(2):
                             for piece, val in enumerate(split3(vals[par])):
-                                vp[slot, par, piece, ch, pl.ds(y1 * 256 + h * 128, 128),
-                                   pl.ds(pair * 128, 128)] = val
+                                vp[slot, par, piece, ch, pair, pl.ds(y1 * 256 + h * 128, 128)] = val
 
         def more_loads(j):
             @pl.when(j + 4 < n)
@@ -230,7 +270,7 @@
                     cp.start()
 
         def gram(j):
-            vh, vm, vl = (vp[slot, kk, piece, 7 - j] for piece in range(3))
+            vh, vm, vl = (part_of(slot, kk, piece, 7 - j) for piece in range(3))
             lhs = jnp.concatenate([vh.T[64:], vm.T[64:], vl.T[64:]], axis=0)
             prod = dot6(lhs, vh, vm, vl, NN)
             gacc[...] += prod
@@ -256,9 +296,7 @@
 
         def panel(e):
             val = tbv[(e // 2 + xx) % 2 * 2 + (e % 2 + kk) % 2, qn]
-            other = pltpu.roll(val, 64, 1)
-            return (jnp.where(left64, jnp.where(kk == 0, val, other), 0.0),
-                    jnp.where(left64, 0.0, jnp.where(kk == 0, other, val)))
+            return val, pltpu.roll(val, 64, 1)
 
         def padded(val):
             return split3(jnp.concatenate([val, zero], axis=0))
@@ -284,17 +322,17 @@
 
     def update(s, slot, par, ch):
         yst = ys[...]
-        delta = dot6(yst, vp[slot, par, 0, ch], vp[slot, par, 1, ch], vp[slot, par, 2, ch], NT)
+        delta = dot6(yst, *(part_of(slot, par, piece, ch) for piece in range(3)), NT)
         new = xt[s, ch] - delta
         xt[s, ch] = new
         return new
 
     def project_half(s, slot, par, ch, t):
         part = pl.ds(256 * t, 256)
-        return dot6(stack3(xt[s, ch, :, part]), *(vp[slot, par, piece, ch, part] for piece in range(3)), NN)
+        return dot6(stack3(xt[s, ch, :, part]), *(part_of(slot, par, piece, ch, part) for piece in range(3)), NN)
 
     def project(s, slot, par, ch):
-        return dot6(stack3(xt[s, ch]), vp[slot, par, 0, ch], vp[slot, par, 1, ch], vp[slot, par, 2, ch], NN)
+        return dot6(stack3(xt[s, ch]), *(part_of(slot, par, piece, ch) for piece in range(3)), NN)
 
     near_half = pl.ds(pl.multiple_of(yy * 256, 256), 256)
     far_half = pl.ds(pl.multiple_of((1 - yy) * 256, 256), 256)
@@ -337,30 +375,34 @@
             def _():
                 at_trip(i, here)
 
-        @pl.when(g == 1)
-        def _():
-            t_copy(0, 1).wait_recv()
-            t_copy(0, 2).start()
-
-        @pl.when(g == 3)
-        def _():
-            t_copy(0, 0).wait_recv()
-            t_copy(0, 2).wait_recv()
-
-        @pl.when(g == REST)
-        def _():
-            t_copy(1, 0).start()
-            t_copy(1, 1).start()
-
-        @pl.when(g == REST + 6)
-        def _():
-            t_copy(1, 1).wait_recv()
-            t_copy(1, 2).start()
-
-        @pl.when(g == REST + 9)
-        def _():
-            t_copy(1, 0).wait_recv()
-            t_copy(1, 2).wait_recv()
+        @pl.when(g < REST + 10)
+        def _():
+            @pl.when(g == 1)
+            def _():
+                t_copy(0, 1).wait_recv()
+                t_copy(0, 2).start()
+
+            @pl.when(g == 3)
+            def _():
+                t_copy(0, 0).wait_recv()
+                t_copy(0, 2).wait_recv()
+                lax.fori_loop(48, 64, unpack, 0)
+
+            @pl.when(g == REST)
+            def _():
+                t_copy(1, 0).start()
+                t_copy(1, 1).start()
+
+            @pl.when(g == REST + 6)
+            def _():
+                t_copy(1, 1).wait_recv()
+                t_copy(1, 2).start()
+
+            @pl.when(g == REST + 9)
+            def _():
+                t_copy(1, 0).wait_recv()
+                t_copy(1, 2).wait_recv()
+                lax.fori_loop(0, 48, unpack, 0)
 
         @pl.when((sub == 0) & more)
         def _():
@@ -415,101 +457,114 @@
             ys[...] = stack3(y_val)
             y_out[y_at] = y_val
 
-        for chunks in range(1, 9):
-            @pl.when(has_u & has_w & (n == chunks))
+        def both(chunks):
+            solve()
+            totals = [None, None]
+            for j in range(chunks + 1):
+                if j < chunks:
+                    update(s, cur, par, 7 - j)
+                if j > 0:
+                    for t in range(2):
+                        prod = project_half(s, w_slot, w_par, 8 - j, t)
+                        totals[t] = prod if totals[t] is None else totals[t] + prod
+            wsend[s, w_par] = totals[0]
+            whalf[...] = totals[1]
+
+        for first in range(1, 9, 4):
+            @pl.when(has_u & has_w & (n >= first) & (n < first + 4))
+            def _():
+                for chunks in range(first, first + 4):
+                    @pl.when(n == chunks)
+                    def _():
+                        both(chunks)
+
+        @pl.when(has_w)
+        def _():
+            @pl.when(has_u)
+            def _():
+                wsend[s, w_par] += whalf[...]
+
+                @pl.when(n_w > n)
+                def _():
+                    wsend[s, w_par] += project(s, w_slot, w_par, 7 - n)
+
+            @pl.when(jnp.logical_not(has_u))
+            def _():
+                wsend[s, w_par] = project(s, w_slot, w_par, 7)
+            w_copy(s, w_par).start()
+
+        @pl.when((sub == 0) & more)
+        def _():
+            g_copy(nxt).start()
+
+        @pl.when(((sub == 1) | (sub == 2)) & (qn % 2 == 1) & (qn >= 5))
+        def _():
+            z_copy(qn // 2 - 2, sub - 1).start()
+
+        @pl.when(i >= NBLK - 3)
+        def _():
+            @pl.when(tell & has_w)
+            def _():
+                y_copy(y_at).start()
+
+            @pl.when((i == NBLK - 3) & (sub == 3))
+            def _():
+                def keep(ch, _):
+                    early[ch] = xt[1, ch, :, far_half]
+                    return 0
+                lax.fori_loop(0, 8, keep, 0)
+                early_copy().start()
+
+            @pl.when((i == NBLK - 1) & (sub == 2))
             def _():
                 solve()
-                totals = [None, None]
-                for j in range(chunks + 1):
-                    if j < chunks:
-                        update(s, cur, par, 7 - j)
-                    if j > 0:
-                        for t in range(2):
-                            prod = project_half(s, w_slot, w_par, 8 - j, t)
-                            totals[t] = prod if totals[t] is None else totals[t] + prod
-                wsend[s, w_par] = totals[0]
-                whalf[...] = totals[1]
-
-        @pl.when(has_u & has_w)
-        def _():
-            wsend[s, w_par] += whalf[...]
-
-        @pl.when(has_w & jnp.logical_not(has_u))
-        def _():
-            wsend[s, w_par] = project(s, w_slot, w_par, 7)
-
-        @pl.when(has_w & has_u & (n_w > n))
-        def _():
-            wsend[s, w_par] += project(s, w_slot, w_par, 7 - n)
-
-        @pl.when(has_w)
-        def _():
-            w_copy(s, w_par).start()
-
-        @pl.when((sub == 0) & more)
-        def _():
-            g_copy(nxt).start()
-
-        @pl.when(((sub == 1) | (sub == 2)) & (qn % 2 == 1) & (qn >= 5))
-        def _():
-            z_copy(qn // 2 - 2, sub - 1).start()
-
-        @pl.when(tell & has_w)
-        def _():
-            y_copy(y_at).start()
-
-        @pl.when((i == NBLK - 3) & (sub == 3))
-        def _():
-            def keep(ch, _):
-                early[ch] = xt[1, ch, :, far_half]
-                return 0
-            lax.fori_loop(0, 8, keep, 0)
-            early_copy().start()
-
-        @pl.when((i == NBLK - 1) & (sub == 2))
-        def _():
-            solve()
-            update(0, cur, 0, 7)
-
-            def give(ch):
-                osb[ch] = xt[0, ch, :, far_half].T
-                out_copy(ch).start()
-                o[mult_rows(ch), own_cols(0)] = xt[0, ch, :, near_half].T
-
-            def last(j, _):
-                give(8 - j)
-                update(0, cur, 0, 7 - j)
-                return 0
-            lax.fori_loop(1, 8, last, 0)
-            give(0)
-
-        @pl.when((i == NBLK - 1) & (sub == 3))
-        def _():
-            solve()
-            y_copy(3).start()
-
-            def near(pair, _):
-                yst = ys[...]
-                for ch in (2 * pair, 2 * pair + 1):
-                    delta = dot6(yst, *(vp[cur, 0, piece, ch, near_half] for piece in range(3)), NT)
-                    o[mult_rows(ch), own_cols(1)] = (xt[1, ch, :, near_half] - delta).T
-                return 0
-            lax.fori_loop(0, 4, near, 0)
-
-            early_copy().wait_recv()
-            for at in range(4):
-                y_copy(at).wait_recv()
-                yin[at] = stack3(y_in[at])
-
-            def far(pair, _):
-                for ch in (2 * pair, 2 * pair + 1):
-                    total = None
-                    for at in range(4):
-                        part = dot6(yin[at], *(vp[at // 2, 1 - at % 2, piece, ch, near_half] for piece in range(3)), NT)
-                        total = part if total is None else total + part
-                    o[mult_rows(ch), far_cols(1)] = (landed[ch] - total).T
-                return 0
-            lax.fori_loop(0, 4, far, 0)
+                update(0, cur, 0, 7)
+
+                def give(ch):
+                    osb[ch] = xt[0, ch, :, far_half].T
+
+                    @pl.when(ch >= 6)
+                    def _():
+                        out_copy(ch).start()
+                    o[mult_rows(ch), own_cols(0)] = xt[0, ch, :, near_half].T
+
+                def last(j, _):
+                    give(8 - j)
+                    update(0, cur, 0, 7 - j)
+                    return 0
+                lax.fori_loop(1, 8, last, 0)
+                osb[0] = xt[0, 0, :, far_half].T
+                o[mult_rows(0), own_cols(0)] = xt[0, 0, :, near_half].T
+
+            @pl.when((i == NBLK - 1) & (sub == 3))
+            def _():
+                solve()
+                y_copy(3).start()
+                for ch in range(5, -1, -1):
+                    out_copy(ch).start()
+
+                def near(pair, _):
+                    yst = ys[...]
+                    for ch in (2 * pair, 2 * pair + 1):
+                        delta = dot6(yst, *(part_of(cur, 0, piece, ch, near_half) for piece in range(3)), NT)
+                        o[mult_rows(ch), own_cols(1)] = (xt[1, ch, :, near_half] - delta).T
+                    return 0
+                lax.fori_loop(0, 4, near, 0)
+
+                early_copy().wait_recv()
+                for at in range(4):
+                    y_copy(at).wait_recv()
+                    yin[at] = stack3(y_in[at])
+
+                def far(pair, _):
+                    for ch in (2 * pair, 2 * pair + 1):
+                        total = None
+                        for at in range(4):
+                            part = dot6(yin[at], *(part_of(at // 2, 1 - at % 2, piece, ch, near_half) for piece in range(3)), NT)
+                            total = part if total is None else total + part
+                        o[mult_rows(ch), far_cols(1)] = (landed[ch] - total).T
+                    return 0
+                lax.fori_loop(0, 4, far, 0)
         return 0
 
     lax.fori_loop(0, 4 * (NBLK + 1), step, 0)
@@ -519,7 +574,10 @@
             t_copy(half, way).wait_send()
     for qq in range(NBLK):
         for idx in range(7):
-            slab(qq, idx).wait_send()
+            for short in (True, False):
+                @pl.when(sent[idx] == short)
+                def _():
+                    slab(qq, idx, short).wait_send()
 
     early_copy().wait_send()
     for at in range(4):
@@ -546,11 +604,12 @@
             in_specs=[any_spec] * 3,
             out_specs=(pl.BlockSpec(memory_space=pltpu.VMEM), any_spec, any_spec),
             scratch_shapes=[
-                vmem((2, 2, 3, 8, 512, 256), BF16),
+                vmem((2, 2, 3, 8, 2, 512, 128), BF16),
                 vmem((2, 8, 128, 512), F32),
                 vmem((4, 8, 256, 128), F32),
                 vmem((2, 2, 256, 128), F32),
                 vmem((32, 64, 64), F32),
+                vmem((4, NBLK // 2, 72, 128), F32),
                 vmem((4, NBLK, 64, 128), F32),
                 vmem((2, 2, 256, 256), F32),
                 vmem((2, 3, 256, 256), BF16),

time: 387 us -> 375 us (0.969)
  Pallas kernels: 384 us -> 373 us
    pallas_call x1, Pallas kernels: 384 us -> 373 us  [local_apply(): pl.pallas_call(kernel, out_shape=(pltpu.VMEM((2048, 512), F32), jax.Shape...]
where the time goes in v5:
time: 375 us
  Pallas kernels  373 us (99%)
    pallas_call x1, Pallas kernels, local_apply(): pl.pallas_call(kernel, out_shape=(pltpu.VMEM((2048, 512), F32), jax.Shape...  373 us

profile of v5, /device:TPU:0, one launch (start us, length us, event | category | flops | bytes accessed | tf_op | source)
XLA Modules:
  0.0 375.1 jit_solution(4693741223930612645)
XLA Ops:
  0.0 373.1 %shard_map.37 = (f32[2048,512]{1,0:T(8,128)S(1)}, f32[16,7,2048,128]{3,2,1,0:T(8,128)}, f32[2,2048,128]{2,1,0:T(8,128)}) custom-call(f32[2048,2048]{1,0:T(8,128)} %v.1, f32[32,64,64]{2,1,0:T(8,128)} %tt.1, f32[4,2048,128]{2,1,0:T(8,128)} %bitcast.1), custom_call_target="tpu_custom_call" | custom-call | tf_op jit(solution)/shard_map/pallas_call | solution.py:599
  373.1 2.0 copy.5

commit v6 on v5

--- a/solution.py
+++ b/solution.py
@@ -8,12 +8,13 @@
 F32 = jnp.float32
 BF16 = jnp.bfloat16
 MESH = pl.DeviceIdType.MESH
+EARLY = 5
 NBLK = 16
-REST = 0
-OWN = (None, None, None, 4, 0, 4, 6, 9, 11, 20, 21, 21, 35, 36, 44, 51)
-FWD = (None, 0, 3, 6, 6, 8, 19, 15, 17, 26, 32, 31, 40, 47, 49, 56)
-DIAG = (None, 0, 4, 9, 9, 17, 23, 27, 29, 32, 36, 40, 46, 50, 53, 58)
-HERE = (None, 3, 8, 11, 15, 19, 24, 28, 32, 36, 39, 43, 48, 51, 55, 59)
+REST = 7
+OWN = (None, None, None, 2, 3, 0, 6, 13, 10, 23, 24, 20, 32, 39, 44, 52)
+FWD = (None, 0, 0, 4, 6, 17, 12, 18, 17, 29, 33, 34, 37, 48, 50, 57)
+DIAG = (None, 1, 6, 9, 12, 19, 18, 23, 25, 34, 38, 40, 44, 51, 53, 60)
+HERE = (None, 2, 6, 11, 14, 20, 22, 27, 30, 35, 39, 43, 47, 52, 55, 60)
 NT = (((1,), (1,)), ((), ()))
 NN = (((1,), (0,)), ((), ()))
 
@@ -30,11 +31,14 @@
     return jnp.concatenate(split3(val), axis=0)
 
 
-def dot6(stack, b_high, b_mid, b_low, dims):
+def dot6(stack, b_high, b_mid, b_low, dims, low_first=False):
     rows = stack.shape[0] // 3
     o_high = lax.dot_general(stack, b_high, dims, preferred_element_type=F32)
-    o_mid = lax.dot_general(stack[:2 * rows], b_mid, dims, preferred_element_type=F32)
+    if not low_first:
+        o_mid = lax.dot_general(stack[:2 * rows], b_mid, dims, preferred_element_type=F32)
     o_low = lax.dot_general(stack[:rows], b_low, dims, preferred_element_type=F32)
+    if low_first:
+        o_mid = lax.dot_general(stack[:2 * rows], b_mid, dims, preferred_element_type=F32)
     small = (o_high[2 * rows:] + o_mid[rows:]) + o_low
     return o_high[:rows] + ((o_high[rows:2 * rows] + o_mid[:rows]) + small)
 
@@ -52,8 +56,8 @@
     return table
 
 
-def kernel(v, tt, z4, o, vb, zb, vp, xt, stage, zst, traw, tbp, tbv, ts, tp, ys, whalf, wsend, wrecv, gacc, gsend, grecv, osb, early, landed, y_out, y_in, yin,
-           v_s, v_r, z_s, z_r, zl, tb_s, tb_r, tb_l, t_s, t_r, w_s, w_r, g_s, g_r, st_a, st_b, o_s, o_r, e_s, e_r, y_s, y_r):
+def kernel(v, tt, z4, o, vb, zb, vp, xt, stage, zst, traw, tbp, tbv, ts, tp, ys, whalf, wsend, wrecv, gacc, gsend, grecv, osb, early, landed, later, settled, y_out, y_in, yin,
+           v_s, v_r, z_s, z_r, zl, tb_s, tb_r, tb_l, t_s, t_r, w_s, w_r, g_s, g_r, st_a, st_b, o_s, o_r, e_s, e_r, l_s, l_r, y_s, y_r):
     r = lax.axis_index('row')
     c = lax.axis_index('col')
     zz, yy, xx, kk = r // 2, r % 2, c // 2, c % 2
@@ -193,24 +197,24 @@
         tbp[0, pair, pl.ds(64, 8)] = jnp.broadcast_to(diag, (8, 128))
         return 0
 
-    def unpack(at, _):
-        q, src = at // 4, at % 4
-        both = tbp[src, q // 2]
-        both = jnp.where(q % 2 == 1, pltpu.roll(both, 64, 1), both)
-        square, diag = both[:64], both[64:65]
-        even = jnp.where((lane64 < 64) & (row64 >= lane64), square, 0.0)
-        odd = jnp.where(row64 < lane64, square, jnp.where(row64 == lane64, jnp.broadcast_to(diag, (64, 128)), 0.0))
-        odd = jnp.where(lane64 < 64, odd, 0.0)
-        odd = jnp.concatenate([odd, jnp.zeros((64, 128), F32)], axis=0).T[:64]
-        tbv[src, q] = jnp.where(kk == 0, even, odd)
+    def unpack(q, _):
+        for src in range(4):
+            both = tbp[src, q // 2]
+            both = jnp.where(q % 2 == 1, pltpu.roll(both, 64, 1), both)
+            square, diag = both[:64], both[64:65]
+            even = jnp.where((lane64 < 64) & (row64 >= lane64), square, 0.0)
+            odd = jnp.where(row64 < lane64, square, jnp.where(row64 == lane64, jnp.broadcast_to(diag, (64, 128)), 0.0))
+            odd = jnp.where(lane64 < 64, odd, 0.0)
+            odd = jnp.concatenate([odd, jnp.zeros((64, 128), F32)], axis=0).T[:64]
+            tbv[src, q] = jnp.where(kk == 0, even, odd)
         return 0
 
     lax.fori_loop(0, NBLK // 2, pack, 0)
     for y1 in range(2):
         z_copy(6, y1).start()
-    send_own(14)
     for y1 in range(2):
         z_copy(7, y1).start()
+    send_own(14)
     pass_on(15)
     send_own(13)
     pass_diag(15)
@@ -329,7 +333,7 @@
 
     def project_half(s, slot, par, ch, t):
         part = pl.ds(256 * t, 256)
-        return dot6(stack3(xt[s, ch, :, part]), *(part_of(slot, par, piece, ch, part) for piece in range(3)), NN)
+        return dot6(stack3(xt[s, ch, :, part]), *(part_of(slot, par, piece, ch, part) for piece in range(3)), NN, True)
 
     def project(s, slot, par, ch):
         return dot6(stack3(xt[s, ch]), *(part_of(slot, par, piece, ch) for piece in range(3)), NN)
@@ -351,6 +355,9 @@
 
     def early_copy():
         return remote(early, landed, e_s, e_r, dev_y)
+
+    def later_copy():
+        return remote(later, settled, l_s, l_r, dev_y)
 
     def y_copy(at):
         return remote(y_out.at[at], y_in.at[at], y_s.at[at], y_r.at[at], dev_y)
@@ -375,7 +382,7 @@
             def _():
                 at_trip(i, here)
 
-        @pl.when(g < REST + 10)
+        @pl.when(g < 15)
         def _():
             @pl.when(g == 1)
             def _():
@@ -386,7 +393,7 @@
             def _():
                 t_copy(0, 0).wait_recv()
                 t_copy(0, 2).wait_recv()
-                lax.fori_loop(48, 64, unpack, 0)
+                lax.fori_loop(12, 16, unpack, 0)
 
             @pl.when(g == REST)
             def _():
@@ -398,11 +405,11 @@
                 t_copy(1, 1).wait_recv()
                 t_copy(1, 2).start()
 
-            @pl.when(g == REST + 9)
+            @pl.when(g == 14)
             def _():
                 t_copy(1, 0).wait_recv()
                 t_copy(1, 2).wait_recv()
-                lax.fori_loop(0, 48, unpack, 0)
+                lax.fori_loop(0, 12, unpack, 0)
 
         @pl.when((sub == 0) & more)
         def _():
@@ -445,8 +452,8 @@
         w_slot = jnp.where(sub < 2, cur, nxt)
         n_w = jnp.where(sub < 2, n, 8 - qn // 2)
 
-        tell = (i >= NBLK - 2) & (s == 1)
-        y_at = jnp.where(tell, 2 * (i - (NBLK - 2)) + 1 - par, 4)
+        tell = ((i >= NBLK - 2) & (s == 1)) | ((i == NBLK - 1) & (s == 0))
+        y_at = jnp.where(tell, jnp.where(s == 1, 2 * (i - (NBLK - 2)), 4) + 1 - par, 6)
 
         def solve():
             w_copy(s, par).wait()
@@ -515,15 +522,26 @@
                 lax.fori_loop(0, 8, keep, 0)
                 early_copy().start()
 
+            @pl.when((i == NBLK - 2) & (sub == 2))
+            def _():
+                def keep(ch, _):
+                    later[ch - EARLY] = xt[0, ch, :, far_half]
+                    return 0
+                lax.fori_loop(EARLY, 8, keep, 0)
+                later_copy().start()
+
             @pl.when((i == NBLK - 1) & (sub == 2))
             def _():
                 solve()
+                y_copy(5).start()
                 update(0, cur, 0, 7)
 
                 def give(ch):
-                    osb[ch] = xt[0, ch, :, far_half].T
-
-                    @pl.when(ch >= 6)
+                    @pl.when(ch < EARLY)
+                    def _():
+                        osb[ch] = xt[0, ch, :, far_half].T
+
+                    @pl.when((ch < EARLY) & (ch >= EARLY - 2))
                     def _():
                         out_copy(ch).start()
                     o[mult_rows(ch), own_cols(0)] = xt[0, ch, :, near_half].T
@@ -540,7 +558,7 @@
             def _():
                 solve()
                 y_copy(3).start()
-                for ch in range(5, -1, -1):
+                for ch in range(EARLY - 3, -1, -1):
                     out_copy(ch).start()
 
                 def near(pair, _):
@@ -551,20 +569,40 @@
                     return 0
                 lax.fori_loop(0, 4, near, 0)
 
-                early_copy().wait_recv()
-                for at in range(4):
+                def from_y(ch, ats):
+                    total = None
+                    for at in ats:
+                        blk, p1 = (at // 2, 1 - at % 2) if at < 4 else (1, 5 - at)
+                        part = dot6(yin[at], *(part_of(blk, p1, piece, ch, near_half) for piece in range(3)), NT)
+                        total = part if total is None else total + part
+                    return total
+
+                def take_y(at):
                     y_copy(at).wait_recv()
                     yin[at] = stack3(y_in[at])
 
+                early_copy().wait_recv()
+                for at in range(3):
+                    take_y(at)
+
                 def far(pair, _):
                     for ch in (2 * pair, 2 * pair + 1):
-                        total = None
-                        for at in range(4):
-                            part = dot6(yin[at], *(part_of(at // 2, 1 - at % 2, piece, ch, near_half) for piece in range(3)), NT)
-                            total = part if total is None else total + part
-                        o[mult_rows(ch), far_cols(1)] = (landed[ch] - total).T
+                        landed[ch] -= from_y(ch, (0, 1, 2))
                     return 0
                 lax.fori_loop(0, 4, far, 0)
+
+                later_copy().wait_recv()
+                for at in (4, 5):
+                    take_y(at)
+                for ch in range(EARLY, 8):
+                    o[mult_rows(ch), far_cols(0)] = (settled[ch - EARLY] - from_y(ch, (4, 5))).T
+                take_y(3)
+
+                def final(pair, _):
+                    for ch in (2 * pair, 2 * pair + 1):
+                        o[mult_rows(ch), far_cols(1)] = (landed[ch] - from_y(ch, (3,))).T
+                    return 0
+                lax.fori_loop(0, 4, final, 0)
         return 0
 
     lax.fori_loop(0, 4 * (NBLK + 1), step, 0)
@@ -580,15 +618,17 @@
                     slab(qq, idx, short).wait_send()
 
     early_copy().wait_send()
-    for at in range(4):
+    later_copy().wait_send()
+    for at in range(6):
         y_copy(at).wait_send()
 
     def drain(ch, _):
         for y1 in range(2):
             z_copy(ch, y1).wait_send()
-        out_copy(ch).wait()
         return 0
     lax.fori_loop(0, 8, drain, 0)
+    for ch in range(EARLY - 1, -1, -1):
+        out_copy(ch).wait()
 
 
 def solution(mesh):
@@ -623,9 +663,11 @@
                 vmem((8, 256, 128), F32),
                 vmem((8, 128, 256), F32),
                 vmem((8, 128, 256), F32),
-                vmem((5, 128, 256), F32),
-                vmem((4, 128, 256), F32),
-                vmem((4, 384, 256), BF16),
+                vmem((8 - EARLY, 128, 256), F32),
+                vmem((8 - EARLY, 128, 256), F32),
+                vmem((7, 128, 256), F32),
+                vmem((6, 128, 256), F32),
+                vmem((6, 384, 256), BF16),
                 dma((NBLK, 7)), dma((NBLK, 7)),
                 dma((8, 2)), dma((8, 2)), dma((2,)),
                 dma((2, 3)), dma((2, 3)), dma,
@@ -634,7 +676,8 @@
                 dma((2,)), dma((2,)),
                 dma((4,)), dma((4,)),
                 dma((8,)), dma((8,)),
-                dma, dma, dma((4,)), dma((4,)),
+                dma, dma, dma, dma,
+                dma((6,)), dma((6,)),
             ],
             compiler_params=pltpu.CompilerParams(collective_id=0, has_side_effects=True, vmem_limit_bytes=56_000_000),
         )(v_loc, t_loc, z4)

time: 375 us -> 371 us (0.989)
  Pallas kernels: 373 us -> 369 us
    pallas_call x1, Pallas kernels: 373 us -> 369 us  [local_apply(): pl.pallas_call(kernel, out_shape=(pltpu.VMEM((2048, 512), F32), jax.Shape...]
where the time goes in v6:
time: 371 us
  Pallas kernels  369 us (99%)
    pallas_call x1, Pallas kernels, local_apply(): pl.pallas_call(kernel, out_shape=(pltpu.VMEM((2048, 512), F32), jax.Shape...  369 us

profile of v6, /device:TPU:0, one launch (start us, length us, event | category | flops | bytes accessed | tf_op | source)
XLA Modules:
  0.0 370.8 jit_solution(13053717551549584545)
XLA Ops:
  0.0 368.8 %shard_map.37 = (f32[2048,512]{1,0:T(8,128)S(1)}, f32[16,7,2048,128]{3,2,1,0:T(8,128)}, f32[2,2048,128]{2,1,0:T(8,128)}) custom-call(f32[2048,2048]{1,0:T(8,128)} %v.1, f32[32,64,64]{2,1,0:T(8,128)} %tt.1, f32[4,2048,128]{2,1,0:T(8,128)} %bitcast.1), custom_call_target="tpu_custom_call" | custom-call | tf_op jit(solution)/shard_map/pallas_call | solution.py:639
  368.8 2.0 copy.5

commit v7 on v6

--- a/solution.py
+++ b/solution.py
@@ -10,11 +10,11 @@
 MESH = pl.DeviceIdType.MESH
 EARLY = 5
 NBLK = 16
-REST = 7
-OWN = (None, None, None, 2, 3, 0, 6, 13, 10, 23, 24, 20, 32, 39, 44, 52)
-FWD = (None, 0, 0, 4, 6, 17, 12, 18, 17, 29, 33, 34, 37, 48, 50, 57)
-DIAG = (None, 1, 6, 9, 12, 19, 18, 23, 25, 34, 38, 40, 44, 51, 53, 60)
-HERE = (None, 2, 6, 11, 14, 20, 22, 27, 30, 35, 39, 43, 47, 52, 55, 60)
+REST = 6
+OWN = (None, None, None, 1, 4, 5, 1, 7, 10, 20, 19, 27, 33, 40, 43, 52)
+FWD = (None, 0, 5, 5, 6, 14, 16, 17, 24, 26, 27, 34, 38, 47, 50, 57)
+DIAG = (None, 3, 6, 8, 13, 17, 19, 28, 29, 32, 37, 42, 45, 51, 53, 60)
+HERE = (None, 3, 7, 10, 14, 20, 23, 28, 31, 34, 38, 43, 47, 52, 55, 60)
 NT = (((1,), (1,)), ((), ()))
 NN = (((1,), (0,)), ((), ()))
 
@@ -211,16 +211,16 @@
 
     lax.fori_loop(0, NBLK // 2, pack, 0)
     for y1 in range(2):
-        z_copy(6, y1).start()
-    for y1 in range(2):
         z_copy(7, y1).start()
     send_own(14)
     pass_on(15)
     send_own(13)
-    pass_diag(15)
     for way in range(2):
         t_copy(0, way).start()
+    pass_diag(15)
     all_here(15)
+    for y1 in range(2):
+        z_copy(6, y1).start()
 
     lane = lax.broadcasted_iota(jnp.int32, (128, 128), 1)
     left = lane < 64

time: 371 us -> 370 us (level)
  no operation moved by 1% of the time
where the time goes in v7:
time: 370 us; the launch traced here: 369 us
  Pallas kernels  367 us (99%)
    pallas_call x1, Pallas kernels, local_apply(): pl.pallas_call(kernel, out_shape=(pltpu.VMEM((2048, 512), F32), jax.Shape...  367 us

profile of v7, /device:TPU:0, one launch (start us, length us, event | category | flops | bytes accessed | tf_op | source)
XLA Modules:
  0.0 368.9 jit_solution(17051786760570407423)
XLA Ops:
  0.0 366.8 %shard_map.37 = (f32[2048,512]{1,0:T(8,128)S(1)}, f32[16,7,2048,128]{3,2,1,0:T(8,128)}, f32[2,2048,128]{2,1,0:T(8,128)}) custom-call(f32[2048,2048]{1,0:T(8,128)} %v.1, f32[32,64,64]{2,1,0:T(8,128)} %tt.1, f32[4,2048,128]{2,1,0:T(8,128)} %bitcast.1), custom_call_target="tpu_custom_call" | custom-call | tf_op jit(solution)/shard_map/pallas_call | solution.py:639
  366.8 2.0 copy.5
